TPU v7x, 32 devices: a whole 2x2x4 slice. The times are simulated.
32 devices in a mesh: rep: 2 (over x), dp: 16 (over y, z, core).
Axes of the slice: x: 2, y: 2, z: 4, core: 2. Of those that a mesh axis runs over, the one named last changes fastest.
Arguments:
- x: bfloat16 [32, 2048, 768], P(('rep', 'dp')), parts along dimension 0
- dy: bfloat16 [32, 2048, 768], P(('rep', 'dp')), parts along dimension 0
- w_gate: bfloat16 [2, 768, 1792], replicated
- w_up: bfloat16 [2, 768, 1792], replicated
- w_down: bfloat16 [2, 1792, 768], replicated
- m_w_gate: float32 [2, 768, 1792], P(None, 'dp')
- m_w_up: float32 [2, 768, 1792], P(None, 'dp')
- m_w_down: float32 [2, 1792, 768], P(None, 'dp')
- v_w_gate: float32 [2, 768, 1792], P(None, 'dp')
- v_w_up: float32 [2, 768, 1792], P(None, 'dp')
- v_w_down: float32 [2, 1792, 768], P(None, 'dp')
Outputs:
- output 1: bfloat16 [4, 768, 1792], P('rep'), parts along dimension 0
- output 2: bfloat16 [4, 768, 1792], P('rep'), parts along dimension 0
- output 3: bfloat16 [4, 1792, 768], P('rep'), parts along dimension 0
- output 4: float32 [4, 768, 1792], P('rep', 'dp'), parts along dimension 0
- output 5: float32 [4, 768, 1792], P('rep', 'dp'), parts along dimension 0
- output 6: float32 [4, 1792, 768], P('rep', 'dp'), parts along dimension 0
- output 7: float32 [4, 768, 1792], P('rep', 'dp'), parts along dimension 0
- output 8: float32 [4, 768, 1792], P('rep', 'dp'), parts along dimension 0
- output 9: float32 [4, 1792, 768], P('rep', 'dp'), parts along dimension 0
There are 2 independent parts. A program takes and returns all parts, laid end to end along the dimension named above; an argument that names none is the same for every part.
All inputs are finite; a program needn't handle non-finite values.
Results may differ from a plain program's by a relative error of at most 0.022.
Values are sent between devices in bfloat16 or wider.
A program may use at most 2 GiB of HBM per device.

v0:
```python
import jax
import jax.numpy as jnp
from jax import lax

NAMES = ("w_gate", "w_up", "w_down")


def matmul(a, w):
    return jnp.dot(a, w, preferred_element_type=jnp.float32).astype(jnp.bfloat16)


def normed(h):
    wide = h.astype(jnp.float32)
    scale = lax.rsqrt(jnp.mean(wide**2, -1, keepdims=True) + 1e-6)
    return (wide * scale).astype(jnp.bfloat16)


def layer(h, w):
    a = normed(h)
    gate = jnp.dot(a, w["w_gate"], preferred_element_type=jnp.float32)
    up = jnp.dot(a, w["w_up"], preferred_element_type=jnp.float32)
    return h + matmul((jax.nn.silu(gate) * up).astype(jnp.bfloat16), w["w_down"])


def adamw(w, m, v, g):
    m = 0.9 * m + 0.1 * g
    v = 0.95 * v + 0.05 * g * g
    step = m * lax.rsqrt(v + 1e-8) + 0.1 * w
    return (w - 0.02 * step).astype(jnp.bfloat16), m, v


def clipped(gradients, sum_of_squares, count):
    factor = jnp.minimum(1.0, 0.5 * lax.rsqrt(sum_of_squares / count + 1e-30))
    return [g * factor for g in gradients]


def stack(weights, h):
    for number in range(weights["w_gate"].shape[0]):
        h = layer(h, {name: w[number] for name, w in weights.items()})
    return h


def solution(mesh):
    groups = mesh.shape["rep"]

    def step(x, dy, *arrays):
        weights, m, v = (arrays[i : i + 3] for i in (0, 3, 6))
        x, dy = (t.reshape(groups, -1, *t.shape[1:]) for t in (x, dy))

        def of_a_group(x, dy):
            _, back = jax.vjp(lambda w: stack(w, x), dict(zip(NAMES, weights, strict=True)))
            by_weights = back(dy)[0]
            gradients = [by_weights[name].astype(jnp.float32) for name in NAMES]
            gradients = clipped(gradients, sum(jnp.sum(g * g) for g in gradients), sum(g.size for g in gradients))
            new = [adamw(w.astype(jnp.float32), m, v, g) for w, m, v, g in zip(weights, m, v, gradients, strict=True)]
            return tuple(one[which] for which in range(3) for one in new)

        return tuple(t.reshape(-1, *t.shape[2:]) for t in jax.vmap(of_a_group)(x, dy))

    return step
```

profile of v0, /device:TPU:0, one launch (start us, length us, event | category | flops | bytes accessed | tf_op | source)
XLA Modules:
  0.0 1139.0 jit_solution(7334708549140664266)
XLA Ops:
  17.5 10.5 convolution_convert_fusion.1
  28.0 11.0 fusion.197
  39.1 14.1 %fusion.156 = (bf16[1,1,2048,1792]{3,2,1,0:T(8,128)(2,1)}, f32[2048,1792]{1,0:T(8,128)}) fusion(f32[2048,1792]{1,0:T(8,128)} %fusion.197, bf16[2,768,1792]{2,1,0:T(8,128)(2,1)S(1)} %bitcast.644, bf16[1,2048,768]{2,1,0:T(8,128)(2,1)S(1)} %copy-done.8, f32[2048]{0:T(1024)S(1)} %add_rsqrt_fusion), kind=kOutput, calls=%fused_computation.191 | convolution fusion | flops 5663883264 | bytes 42606592 | tf_op jit(solution)/vmap(jvp())/dot_general | solution.py:21
  53.2 10.7 copy.4
  63.9 9.7 fusion.166
  76.2 12.0 %fusion.183 = f32[2048,1792]{1,0:T(8,128)} fusion(bf16[1,1,2048,768]{2,3,1,0:T(8,128)(2,1)S(1)} %fusion.167, bf16[2,768,1792]{2,1,0:T(8,128)(2,1)} %param.15), kind=kOutput, calls=%fused_computation.225 | convolution fusion | flops 5637144576 | bytes 20578304 | tf_op jit(solution)/vmap(jvp())/dot_general | solution.py:21
  88.2 22.4 %fusion.145 = (bf16[1,1,2048,1792]{3,2,1,0:T(8,128)(2,1)}, bf16[1,1,2048,1792]{3,2,1,0:T(8,128)(2,1)}, f32[2048,1792]{1,0:T(8,128)}) fusion(f32[2048,1792]{1,0:T(8,128)} %fusion.183, bf16[2048,1792]{1,0:T(8,128)(2,1)} %convolution_convert_fusion.1, bf16[2,768,1792]{2,1,0:T(8,128)(2,1)} %param.12, bf16[1,1,2048,768]{2,3,1,0:T(8,128)(2,1)S(1)} %fusion.167), kind=kOutput, calls=%fused_computation.175 | convolution fusion | flops 5692194816 | bytes 57278464 | tf_op jit(solution)/vmap(jvp())/dot_general | solution.py:20
  110.7 9.1 fusion.172
  119.8 18.5 %fusion.168 = (f32[2048]{0:T(1024)S(1)}, bf16[2048,768]{0,1:T(8,128)(2,1)S(1)}) fusion(bf16[1,1,2048,768]{2,3,1,0:T(8,128)(2,1)S(1)} %copy-done.12, bf16[2048,768]{0,1:T(8,128)(2,1)S(1)} %fusion.172, bf16[2,768,1792]{2,1,0:T(8,128)(2,1)} %param.12, bf16[1,1,2048,1792]{3,2,1,0:T(8,128)(2,1)S(1)} %copy-done.4), kind=kOutput, calls=%fused_computation.215 | convolution fusion | flops 5645006848 | bytes 19537920 | tf_op jit(solution)/vmap(transpose(jvp()))/dot_general | solution.py:20
  145.8 113.9 %while.17 = (bf16[1,1,2048,1792]{2,3,1,0:T(8,128)(2,1)}, bf16[1,1,2048,768]{3,2,1,0:T(8,128)(2,1)S(1)}, f32[1,112,768]{2,1,0:T(8,128)S(1)}, f32[1,112,768]{2,1,0...) while((bf16[1,1,2048,1792]{2,3,1,0:T(8,128)(2,1)}, ...), condition=%wide.windowed_dot_general_cond_rs.5.clone, body=%wide.windowed_dot_general_body_rs.5.clone.sunk | while | flops 1413472256 | bytes 33358436 | solution.py:9
  259.7 13.3 %fusion.155 = bf16[1,1,2048,1792]{3,2,1,0:T(8,128)(2,1)} fusion(f32[2048,1792]{1,0:T(8,128)} %fusion.183, f32[2048,1792]{1,0:T(8,128)} %get-tuple-element.267), kind=kLoop, calls=%fused_computation.189 | loop fusion | flops 22020096 | bytes 36700160 | tf_op jit(solution)/vmap(jvp())/convert_element_type | solution.py:22
  273.1 10.6 copy.2
  286.9 115.8 %while.16 = (bf16[1,1,2048,1792]{2,3,1,0:T(8,128)(2,1)}, bf16[1,1,2048,768]{3,2,1,0:T(8,128)(2,1)S(1)}, f32[1,112,768]{2,1,0:T(8,128)S(1)}, f32[1,112,768]{2,1,0...) while((bf16[1,1,2048,1792]{2,3,1,0:T(8,128)(2,1)}, ...), condition=%wide.windowed_dot_general_cond_rs.4.clone, body=%wide.windowed_dot_general_body_rs.4.clone.sunk | while | flops 1413472256 | bytes 33358436 | solution.py:9
  308.1 5.8 collective-permute-done.18
  407.4 19.5 %convert_multiply_fusion = (bf16[1,1,2048,1792]{3,2,1,0:T(8,128)(2,1)}, bf16[1,1,2048,1792]{3,2,1,0:T(8,128)(2,1)}) fusion(f32[2048,1792]{1,0:T(8,128)} %fusion.197, f32[2048,1792]{1,0:T(8,128)} %get-tuple-element.264, bf16[2,1792,768]{2,1,0:T(8,128)(2,1)} %param.16, bf16[1,1,2048,768]{2,3,1,0:T(8,128)(2,1)S(1)} %copy-done.10), kind=kOutput, calls=%fused_computation.170 | convolution fusion | flops 5695864832 | bytes 49938432 | tf_op jit(solution)/vmap(transpose(jvp()))/dot_general | solution.py:9
  426.9 116.6 %while.15 = (bf16[1,1,2048,768]{2,3,1,0:T(8,128)(2,1)}, bf16[1,1,2048,1792]{3,2,1,0:T(8,128)(2,1)}, f32[1,48,1792]{2,1,0:T(8,128)}, f32[1,48,1792]{2,1,0:T(8,128...) while((bf16[1,1,2048,768]{2,3,1,0:T(8,128)(2,1)}, ...), condition=%wide.windowed_dot_general_cond_rs.3.clone, body=%wide.windowed_dot_general_body_rs.3.clone.sunk | while | flops 1411375104 | bytes 75301536 | solution.py:21
  543.6 116.0 %while.14 = (bf16[1,1,2048,768]{2,3,1,0:T(8,128)(2,1)S(1)}, bf16[1,1,2048,1792]{3,2,1,0:T(8,128)(2,1)}, f32[1,48,1792]{2,1,0:T(8,128)}, f32[1,48,1792]{2,1,0:T(8...) while((bf16[1,1,2048,768]{2,3,1,0:T(8,128)(2,1)S(1)}, ...), condition=%wide.windowed_dot_general_cond_rs.2.clone, body=%wide.windowed_dot_general_body_rs.2.clone.sunk | while | flops 1411375104 | bytes 33358436 | solution.py:21
  659.5 121.1 %while.13 = (bf16[1,1,2048,768]{2,3,1,0:T(8,128)(2,1)}, bf16[1,1,2048,1792]{3,2,1,0:T(8,128)(2,1)}, f32[1,48,1792]{2,1,0:T(8,128)}, f32[1,48,1792]{2,1,0:T(8,128...) while((bf16[1,1,2048,768]{2,3,1,0:T(8,128)(2,1)}, ...), condition=%wide.windowed_dot_general_cond_rs.1.clone, body=%wide.windowed_dot_general_body_rs.1.clone.sunk | while | flops 1411375104 | bytes 75301536 | solution.py:20
  780.6 111.9 %while.12 = (bf16[1,1,2048,768]{2,3,1,0:T(8,128)(2,1)S(1)}, bf16[1,1,2048,1792]{3,2,1,0:T(8,128)(2,1)}, f32[1,48,1792]{2,1,0:T(8,128)S(1)}, f32[1,48,1792]{2,1,0...) while((bf16[1,1,2048,768]{2,3,1,0:T(8,128)(2,1)S(1)}, ...), condition=%wide.windowed_dot_general_cond_rs.clone, body=%wide.windowed_dot_general_body_rs.clone.sunk | while | flops 1411375104 | bytes 33358436 | solution.py:20
  912.2 30.6 %all-reduce.10 = f32[1]{0:T(128)} all-reduce(f32[1]{0:T(128)} %bitcast.39), channel_id=13, replica_groups=mesh['rep'=2,'dp'=16] {'dp'}, use_global_device_ids=true, to_apply=%region_3.4.clone | all-reduce | flops 1 | bytes 8 | tf_op jit(solution)/vmap()/reduce_sum | solution.py:54
  952.1 50.4 %all-gather.14.cloned.1.call-done = bf16[1,2,1792,768]{3,2,1,0:T(8,128)(2,1)} async-done(((bf16[1,2,112,768]{3,2,1,0:T(8,128)(2,1)}), bf16[1,2,1792,768]{3,2,1,0:T(8,128)(2,1)}) %all-gather.14.cloned.1.call-update) | async-done | bytes 5505040 | tf_op jit(solution)/reshape | solution.py:58
  1002.5 58.6 %all-gather.12.cloned.1.call-done = bf16[1,2,768,1792]{3,2,1,0:T(8,128)(2,1)} async-done(((bf16[1,2,48,1792]{3,2,1,0:T(8,128)(2,1)}), bf16[1,2,768,1792]{3,2,1,0:T(8,128)(2,1)}) %all-gather.12.cloned.1.call-update) | async-done | bytes 5505040 | tf_op jit(solution)/reshape | solution.py:58
  1061.1 58.6 %all-gather.10.cloned.1.call-done = bf16[1,2,768,1792]{3,2,1,0:T(8,128)(2,1)} async-done(((bf16[1,2,48,1792]{3,2,1,0:T(8,128)(2,1)}), bf16[1,2,768,1792]{3,2,1,0:T(8,128)(2,1)}) %all-gather.10.cloned.1.call-update) | async-done | bytes 5505040 | tf_op jit(solution)/reshape | solution.py:58
  1119.7 5.9 copy.63
  (500 shorter events, 701.5 us)
Async XLA Ops:
  7.2 995.3 %all-gather.14.cloned.1.call-start = ((), (), s32[]{:S(2)}) async-start(), calls=%async_computation.2 | async-start | bytes 5849088 | tf_op jit(solution)/reshape | solution.py:58
  173.9 12.9 %collective-permute-start.20 = (f32[1,112,768]{2,1,0:T(8,128)}, f32[1,112,768]{2,1,0:T(8,128)}, u32[]{:S(2)}, u32[]{:S(2)}) collective-permute-start(f32[1,112,768]{2,1,0:T(8,128)} %broadcast_select_fusion.34), channel_id=35, source_target_pairs={{0,1},{1,2},{2,3},{3,4},{4,5},{5,6},{6,7},{7,8},{8,9},{9,10},{10,1... | collective-permute-start | bytes 1032200 | tf_op jit(solution)/vmap(transpose(jvp()))/dot_general | solution.py:9
  216.9 12.9 %collective-permute-start.23 = (f32[1,112,768]{2,1,0:T(8,128)S(1)}, f32[1,112,768]{2,1,0:T(8,128)S(1)}, u32[]{:S(2)}, u32[]{:S(2)}) collective-permute-start(f32[1,112,768]{2,1,0:T(8,128)S(1)} %get-tuple-element.501), channel_id=36, source_target_pairs={{0,15},{1,0},{2,1},{3,2},{4,3},{5,4},{6,5},{7,6},{8,7},{9,8},{10,9... | collective-permute-start | bytes 1032200 | tf_op jit(solution)/vmap(transpose(jvp()))/dot_general | solution.py:9
  259.7 634.1 %collective-permute-start.29 = (f32[1,112,768]{2,1,0:T(8,128)}, f32[1,112,768]{2,1,0:T(8,128)}, u32[]{:S(2)}, u32[]{:S(2)}) collective-permute-start(f32[1,112,768]{2,1,0:T(8,128)} %get-tuple-element.47), channel_id=38, source_target_pairs={{0,1},{1,2},{2,3},{3,4},{4,5},{5,6},{6,7},{7,8},{8,9},{9,10},{10,1... | collective-permute-start | bytes 1032200 | tf_op jit(solution)/vmap(transpose(jvp()))/dot_general | solution.py:9
  330.1 13.0 %collective-permute-start.19 = (f32[1,112,768]{2,1,0:T(8,128)S(1)}, f32[1,112,768]{2,1,0:T(8,128)S(1)}, u32[]{:S(2)}, u32[]{:S(2)}) collective-permute-start(f32[1,112,768]{2,1,0:T(8,128)S(1)} %get-tuple-element.492), channel_id=30, source_target_pairs={{0,15},{1,0},{2,1},{3,2},{4,3},{5,4},{6,5},{7,6},{8,7},{9,8},{10,9... | collective-permute-start | bytes 1032200 | tf_op jit(solution)/vmap(transpose(jvp()))/dot_general | solution.py:9
  359.7 13.1 %collective-permute-start.19 = (f32[1,112,768]{2,1,0:T(8,128)S(1)}, f32[1,112,768]{2,1,0:T(8,128)S(1)}, u32[]{:S(2)}, u32[]{:S(2)}) collective-permute-start(f32[1,112,768]{2,1,0:T(8,128)S(1)} %get-tuple-element.492), channel_id=30, source_target_pairs={{0,15},{1,0},{2,1},{3,2},{4,3},{5,4},{6,5},{7,6},{8,7},{9,8},{10,9... | collective-permute-start | bytes 1032200 | tf_op jit(solution)/vmap(transpose(jvp()))/dot_general | solution.py:9
  402.8 492.3 %collective-permute-start.28 = (f32[1,112,768]{2,1,0:T(8,128)}, f32[1,112,768]{2,1,0:T(8,128)}, u32[]{:S(2)}, u32[]{:S(2)}) collective-permute-start(f32[1,112,768]{2,1,0:T(8,128)} %get-tuple-element.45), channel_id=32, source_target_pairs={{0,1},{1,2},{2,3},{3,4},{4,5},{5,6},{6,7},{7,8},{8,9},{9,10},{10,1... | collective-permute-start | bytes 1032200 | tf_op jit(solution)/vmap(transpose(jvp()))/dot_general | solution.py:9
  454.7 13.5 %collective-permute-start.12 = (f32[1,48,1792]{2,1,0:T(8,128)S(1)}, f32[1,48,1792]{2,1,0:T(8,128)}, u32[]{:S(2)}, u32[]{:S(2)}) collective-permute-start(f32[1,48,1792]{2,1,0:T(8,128)S(1)} %broadcast_select_fusion.30), channel_id=22, source_target_pairs={{0,1},{1,2},{2,3},{3,4},{4,5},{5,6},{6,7},{7,8},{8,9},{9,10},{10,1... | collective-permute-start | bytes 1032200 | tf_op jit(solution)/vmap(transpose(jvp()))/dot_general | solution.py:21
  484.5 13.7 %collective-permute-start.12 = (f32[1,48,1792]{2,1,0:T(8,128)S(1)}, f32[1,48,1792]{2,1,0:T(8,128)}, u32[]{:S(2)}, u32[]{:S(2)}) collective-permute-start(f32[1,48,1792]{2,1,0:T(8,128)S(1)} %broadcast_select_fusion.30), channel_id=22, source_target_pairs={{0,1},{1,2},{2,3},{3,4},{4,5},{5,6},{6,7},{7,8},{8,9},{9,10},{10,1... | collective-permute-start | bytes 1032200 | tf_op jit(solution)/vmap(transpose(jvp()))/dot_general | solution.py:21
  514.3 13.7 %collective-permute-start.12 = (f32[1,48,1792]{2,1,0:T(8,128)S(1)}, f32[1,48,1792]{2,1,0:T(8,128)}, u32[]{:S(2)}, u32[]{:S(2)}) collective-permute-start(f32[1,48,1792]{2,1,0:T(8,128)S(1)} %broadcast_select_fusion.30), channel_id=22, source_target_pairs={{0,1},{1,2},{2,3},{3,4},{4,5},{5,6},{6,7},{7,8},{8,9},{9,10},{10,1... | collective-permute-start | bytes 1032200 | tf_op jit(solution)/vmap(transpose(jvp()))/dot_general | solution.py:21
  529.8 12.9 %collective-permute-start.15 = (f32[1,48,1792]{2,1,0:T(8,128)S(1)}, f32[1,48,1792]{2,1,0:T(8,128)S(1)}, u32[]{:S(2)}, u32[]{:S(2)}) collective-permute-start(f32[1,48,1792]{2,1,0:T(8,128)S(1)} %get-tuple-element.483), channel_id=23, source_target_pairs={{0,15},{1,0},{2,1},{3,2},{4,3},{5,4},{6,5},{7,6},{8,7},{9,8},{10,9... | collective-permute-start | bytes 1032200 | tf_op jit(solution)/vmap(transpose(jvp()))/dot_general | solution.py:21
  543.5 353.4 %collective-permute-start.27 = (f32[1,48,1792]{2,1,0:T(8,128)}, f32[1,48,1792]{2,1,0:T(8,128)}, u32[]{:S(2)}, u32[]{:S(2)}) collective-permute-start(f32[1,48,1792]{2,1,0:T(8,128)} %get-tuple-element.43), channel_id=25, source_target_pairs={{0,1},{1,2},{2,3},{3,4},{4,5},{5,6},{6,7},{7,8},{8,9},{9,10},{10,1... | collective-permute-start | bytes 1032200 | tf_op jit(solution)/vmap(transpose(jvp()))/dot_general | solution.py:21
  544.6 15.4 %collective-permute-start.8 = (f32[1,48,1792]{2,1,0:T(8,128)}, f32[1,48,1792]{2,1,0:T(8,128)}, u32[]{:S(2)}, u32[]{:S(2)}) collective-permute-start(f32[1,48,1792]{2,1,0:T(8,128)} %broadcast_select_fusion.28), channel_id=16, source_target_pairs={{0,1},{1,2},{2,3},{3,4},{4,5},{5,6},{6,7},{7,8},{8,9},{9,10},{10,1... | collective-permute-start | bytes 1032200 | tf_op jit(solution)/vmap(transpose(jvp()))/dot_general | solution.py:21
  545.3 14.6 %collective-permute-start.9 = (f32[1,48,1792]{2,1,0:T(8,128)}, f32[1,48,1792]{2,1,0:T(8,128)}, u32[]{:S(2)}, u32[]{:S(2)}) collective-permute-start(f32[1,48,1792]{2,1,0:T(8,128)} %broadcast_select_fusion.29), channel_id=15, source_target_pairs={{0,15},{1,0},{2,1},{3,2},{4,3},{5,4},{6,5},{7,6},{8,7},{9,8},{10,9... | collective-permute-start | bytes 1032200 | tf_op jit(solution)/vmap(transpose(jvp()))/dot_general | solution.py:21
  575.1 13.3 %collective-permute-start.8 = (f32[1,48,1792]{2,1,0:T(8,128)}, f32[1,48,1792]{2,1,0:T(8,128)}, u32[]{:S(2)}, u32[]{:S(2)}) collective-permute-start(f32[1,48,1792]{2,1,0:T(8,128)} %broadcast_select_fusion.28), channel_id=16, source_target_pairs={{0,1},{1,2},{2,3},{3,4},{4,5},{5,6},{6,7},{7,8},{8,9},{9,10},{10,1... | collective-permute-start | bytes 1032200 | tf_op jit(solution)/vmap(transpose(jvp()))/dot_general | solution.py:21
  603.8 13.3 %collective-permute-start.8 = (f32[1,48,1792]{2,1,0:T(8,128)}, f32[1,48,1792]{2,1,0:T(8,128)}, u32[]{:S(2)}, u32[]{:S(2)}) collective-permute-start(f32[1,48,1792]{2,1,0:T(8,128)} %broadcast_select_fusion.28), channel_id=16, source_target_pairs={{0,1},{1,2},{2,3},{3,4},{4,5},{5,6},{6,7},{7,8},{8,9},{9,10},{10,1... | collective-permute-start | bytes 1032200 | tf_op jit(solution)/vmap(transpose(jvp()))/dot_general | solution.py:21
  632.5 13.3 %collective-permute-start.8 = (f32[1,48,1792]{2,1,0:T(8,128)}, f32[1,48,1792]{2,1,0:T(8,128)}, u32[]{:S(2)}, u32[]{:S(2)}) collective-permute-start(f32[1,48,1792]{2,1,0:T(8,128)} %broadcast_select_fusion.28), channel_id=16, source_target_pairs={{0,1},{1,2},{2,3},{3,4},{4,5},{5,6},{6,7},{7,8},{8,9},{9,10},{10,1... | collective-permute-start | bytes 1032200 | tf_op jit(solution)/vmap(transpose(jvp()))/dot_general | solution.py:21
  690.0 13.8 %collective-permute-start.4 = (f32[1,48,1792]{2,1,0:T(8,128)}, f32[1,48,1792]{2,1,0:T(8,128)}, u32[]{:S(2)}, u32[]{:S(2)}) collective-permute-start(f32[1,48,1792]{2,1,0:T(8,128)} %broadcast_select_fusion.26), channel_id=9, source_target_pairs={{0,1},{1,2},{2,3},{3,4},{4,5},{5,6},{6,7},{7,8},{8,9},{9,10},{10,1... | collective-permute-start | bytes 1032200 | tf_op jit(solution)/vmap(transpose(jvp()))/dot_general | solution.py:20
  721.0 13.8 %collective-permute-start.4 = (f32[1,48,1792]{2,1,0:T(8,128)}, f32[1,48,1792]{2,1,0:T(8,128)}, u32[]{:S(2)}, u32[]{:S(2)}) collective-permute-start(f32[1,48,1792]{2,1,0:T(8,128)} %broadcast_select_fusion.26), channel_id=9, source_target_pairs={{0,1},{1,2},{2,3},{3,4},{4,5},{5,6},{6,7},{7,8},{8,9},{9,10},{10,1... | collective-permute-start | bytes 1032200 | tf_op jit(solution)/vmap(transpose(jvp()))/dot_general | solution.py:20
  752.0 13.8 %collective-permute-start.4 = (f32[1,48,1792]{2,1,0:T(8,128)}, f32[1,48,1792]{2,1,0:T(8,128)}, u32[]{:S(2)}, u32[]{:S(2)}) collective-permute-start(f32[1,48,1792]{2,1,0:T(8,128)} %broadcast_select_fusion.26), channel_id=9, source_target_pairs={{0,1},{1,2},{2,3},{3,4},{4,5},{5,6},{6,7},{7,8},{8,9},{9,10},{10,1... | collective-permute-start | bytes 1032200 | tf_op jit(solution)/vmap(transpose(jvp()))/dot_general | solution.py:20
  837.9 12.9 %collective-permute-start = (f32[1,48,1792]{2,1,0:T(8,128)}, f32[1,48,1792]{2,1,0:T(8,128)}, u32[]{:S(2)}, u32[]{:S(2)}) collective-permute-start(f32[1,48,1792]{2,1,0:T(8,128)} %broadcast_select_fusion.24), channel_id=3, source_target_pairs={{0,1},{1,2},{2,3},{3,4},{4,5},{5,6},{6,7},{7,8},{8,9},{9,10},{10,1... | collective-permute-start | bytes 1032200 | tf_op jit(solution)/vmap(transpose(jvp()))/dot_general | solution.py:20
  893.9 15.6 %collective-permute-start.24 = (f32[1,48,1792]{2,1,0:T(8,128)}, f32[1,48,1792]{2,1,0:T(8,128)S(1)}, u32[]{:S(2)}, u32[]{:S(2)}) collective-permute-start(f32[1,48,1792]{2,1,0:T(8,128)} %get-tuple-element.37), channel_id=6, source_target_pairs={{0,1},{1,2},{2,3},{3,4},{4,5},{5,6},{6,7},{7,8},{8,9},{9,10},{10,1... | collective-permute-start | bytes 1032200 | tf_op jit(solution)/vmap(transpose(jvp()))/dot_general | solution.py:20
  946.1 114.9 %all-gather.12.cloned.1.call-start = ((), (), s32[]{:S(2)}) async-start(), calls=%async_computation.1 | async-start | bytes 5849088 | tf_op jit(solution)/reshape | solution.py:58
  949.0 170.7 %all-gather.10.cloned.1.call-start = ((), (), s32[]{:S(2)}) async-start(), calls=%async_computation | async-start | bytes 5849088 | tf_op jit(solution)/reshape | solution.py:58
  (122 other events, 1729.3 us)
Sparse Core Ops, SparseCore 0:
  946.3 56.1 all-gather.13
  1005.3 55.7 all-gather.11
  1063.9 55.7 all-gather.9
where the time goes:
time: 1150 us; the launch traced here: 1140 us
  waiting for transfers between devices  327 us (28%)
  matrix products  277 us (24%)
  starting transfers between devices  220 us (19%)
  other arithmetic  154 us (13%)
  local copies, waits for them, and re-layouts  64.5 us (6%)
  loops' own time  48.2 us (4%)
  blocking collectives  30.6 us (3%)
  between operations  17.8 us (2%)
    reshape x3, waiting for transfers between devices, step(): t.reshape(-1, *t.shape[2:])  168 us
    dot_general x19, matrix products, layer(): gate = jnp.dot(a, w['w_gate'], preferred_element_type=jnp.float32)  111 us
    dot_general x19, matrix products, layer(): up = jnp.dot(a, w['w_up'], preferred_element_type=jnp.float32)  94.2 us
    dot_general x34, starting transfers between devices, matmul(): jnp.dot(a, w, preferred_element_type=jnp.float32).astype(jnp.bfloat16)  75 us
    dot_general x34, starting transfers between devices, layer(): gate = jnp.dot(a, w['w_gate'], preferred_element_type=jnp.float32)  72.3 us
    dot_general x19, matrix products, matmul(): jnp.dot(a, w, preferred_element_type=jnp.float32).astype(jnp.bfloat16)  72.2 us
    dot_general x34, starting transfers between devices, layer(): up = jnp.dot(a, w['w_up'], preferred_element_type=jnp.float32)  72.2 us
    dot_general x34, waiting for transfers between devices, matmul(): jnp.dot(a, w, preferred_element_type=jnp.float32).astype(jnp.bfloat16)  68.7 us
  transfers between devices with their start and end apart: 105, of which 60 were waited for; matrix products, arithmetic and copies ran while one was open for 29% of the time, Pallas kernels for 0%

commit v1 on v0

v1 whole, which is shorter than its diff:
```python
import functools

import jax
import jax.numpy as jnp
from jax import lax
from jax.experimental import pallas as pl
from jax.experimental.pallas import tpu as pltpu
from jax.sharding import PartitionSpec as P

MESH = pl.DeviceIdType.MESH
Y, Z, C = 2, 4, 2
N = Y * Z * C
F32, BF16 = jnp.float32, jnp.bfloat16


def place():
    me = lax.axis_index("dp")
    return me, me // (Z * C), lax.rem(me // C, Z), lax.rem(me, C)


def index(y, z, c):
    return (y * Z + z) * C + c


def remote(src, dst, send, recv, to):
    return pltpu.make_async_remote_copy(
        src_ref=src, dst_ref=dst, send_sem=send, recv_sem=recv, device_id={"dp": to}, device_id_type=MESH
    )


def update_kernel(count, layers, *refs):
    g, m, v, wf = refs[0:3], refs[3:6], refs[6:9], refs[9:12]
    w_out, m_out, v_out = refs[12:15], refs[15:18], refs[18:21]
    full, own, norms = refs[21:24], refs[24:27], refs[27]
    in_sem, norm_send, norm_recv, send_z, recv_z, send_y, recv_y, send_c, recv_c, out_sem = refs[28:]
    me, y, z, c = place()
    rows = [ref.shape[1] for ref in g]
    loads = []
    for i in range(3):
        loads.append(pltpu.make_async_copy(wf[i].at[:, pl.ds(me * rows[i], rows[i])], own[i], in_sem.at[i]))
        loads[-1].start()

    barrier = pltpu.get_barrier_semaphore()

    def hello(d, _):
        pl.semaphore_signal(barrier, inc=1, device_id={"dp": lax.rem(me + d, N)}, device_id_type=MESH)
        return 0

    lax.fori_loop(1, N, hello, 0)

    total = jnp.zeros((), F32)
    for i in range(3):
        columns = g[i].shape[2]

        def squares(t, acc):
            for l in range(layers):
                part = g[i][l, pl.ds(pl.multiple_of(t * 16, 16), 16), :].astype(F32)
                acc = acc + part * part
            return acc

        acc = lax.fori_loop(0, rows[i] // 16, squares, jnp.zeros((16, columns), F32))
        total = total + jnp.sum(acc)
    norms[pl.ds(me, 1)] = jnp.full((1, 8, 128), total, F32)
    pl.semaphore_wait(barrier, N - 1)

    def tell(d):
        to = lax.rem(me + d, N)
        return remote(norms.at[pl.ds(me, 1)], norms.at[pl.ds(me, 1)], norm_send.at[d], norm_recv.at[d], to)

    lax.fori_loop(1, N, lambda d, _: (tell(d).start(), 0)[1], 0)

    def heard(d, _):
        frm = lax.rem(me + N - d, N)
        copy = remote(norms.at[pl.ds(frm, 1)], norms.at[pl.ds(frm, 1)], norm_send.at[d], norm_recv.at[d], frm)
        copy.wait_recv()
        return 0

    lax.fori_loop(1, N, heard, 0)
    sum_of_squares = jnp.sum(norms[...], axis=0)
    factor = jnp.minimum(1.0, 0.5 * lax.rsqrt(sum_of_squares / count + 1e-30))[0:1, 0:1]
    for load in loads:
        load.wait()
    chunks = [(i, l) for l in range(layers) for i in range(3)]
    mixed = {len(chunks) - 1}

    for i, l in chunks:

        def adamw(t, _):
            at = pl.ds(pl.multiple_of(t * 16, 16), 16)
            grad = g[i][l, at, :].astype(F32) * factor
            w = own[i][l, at, :].astype(F32)
            mm = 0.9 * m[i][l, at, :] + 0.1 * grad
            vv = 0.95 * v[i][l, at, :] + 0.05 * grad * grad
            m_out[i][l, at, :] = mm
            v_out[i][l, at, :] = vv
            new = (w - 0.02 * (mm * lax.rsqrt(vv + 1e-8) + 0.1 * w)).astype(BF16)
            full[i][l, pl.ds(pl.multiple_of(me * rows[i] + t * 16, 16), 16), :] = new
            return 0

        lax.fori_loop(0, rows[i] // 16, adamw, 0)

    def block(k, yy, zz, cc):
        i, l = chunks[k]
        return full[i].at[l, pl.ds(index(yy, zz, cc) * rows[i], rows[i])]

    def origin(slot):
        return z - slot if slot < 4 else z + slot - 3

    def has(slot):
        if slot == 0:
            return z >= 0
        return z >= slot if slot < 4 else z + slot - 3 < Z

    def to_y(k, slot):
        ref = block(k, y, origin(slot), c)
        return remote(ref, ref, send_y.at[k, slot], recv_y.at[k, slot], index(1 - y, z, c))

    def from_y(k, slot):
        ref = block(k, 1 - y, origin(slot), c)
        return remote(ref, ref, send_y.at[k, slot], recv_y.at[k, slot], index(1 - y, z, c))

    def to_c(k, side, slot):
        ref = block(k, y if side == 0 else 1 - y, origin(slot), c)
        return remote(ref, ref, send_c.at[k, side, slot], recv_c.at[k, side, slot], index(y, z, 1 - c))

    def from_c(k, side, slot):
        ref = block(k, y if side == 0 else 1 - y, origin(slot), 1 - c)
        return remote(ref, ref, send_c.at[k, side, slot], recv_c.at[k, side, slot], index(y, z, 1 - c))

    lanes = [(k, 0) for k in range(len(chunks))] + [(k, 1) for k in sorted(mixed)]

    def line(n, slot, up):
        k, side = lanes[n]
        ref = block(k, y if side == 0 else 1 - y, origin(slot), c)
        hop = (slot if slot else 0) if up else (slot - 3 if slot else 0)
        return remote(ref, ref, send_z.at[n, 0 if up else 1, hop], recv_z.at[n, 0 if up else 1, hop],
                      index(y, jnp.minimum(z + 1, Z - 1) if up else jnp.maximum(z - 1, 0), c))

    def arrived(n, slot):
        k, side = lanes[n]
        up = slot < 4
        ref = block(k, y if side == 0 else 1 - y, origin(slot), c)
        hop = slot - 1 if up else slot - 4
        return remote(ref, ref, send_z.at[n, 0 if up else 1, hop], recv_z.at[n, 0 if up else 1, hop],
                      index(y, jnp.maximum(z - 1, 0) if up else jnp.minimum(z + 1, Z - 1), c))

    def when(ok, f):
        pl.when(ok)(f)

    waits = []

    def launch(ok, copy):
        when(ok, lambda: copy().start())
        waits.append((ok, copy))

    def spread(n, slot):
        k, side = lanes[n]
        ok = has(slot)
        if slot < 4:
            launch(ok & (z < Z - 1), lambda: line(n, slot, True))
        if slot == 0 or slot >= 4:
            launch(ok & (z > 0), lambda: line(n, slot, False))
        if side == 0 and (k not in mixed or slot == 0):
            launch(ok, lambda: to_y(k, slot))
        launch(ok, lambda: to_c(k, side, slot))

    order = sorted(range(len(chunks)), key=lambda k: k not in mixed)
    for k in order:
        spread(k, 0)
    for k in sorted(mixed):
        from_y(k, 0).wait_recv()
        spread(lanes.index((k, 1)), 0)
    ranked = sorted(range(len(lanes)), key=lambda n: lanes[n][0] not in mixed)
    for hop in range(1, Z):
        for n in ranked:
            for slot in (hop, hop + 3):
                when(has(slot), lambda: arrived(n, slot).wait_recv())
                spread(n, slot)

    def out(k, side):
        i, l = chunks[k]
        half = pl.ds((y if side == 0 else 1 - y) * (Z * C * rows[i]), Z * C * rows[i])
        return pltpu.make_async_copy(full[i].at[l, half], w_out[i].at[l, half], out_sem.at[k, side])

    slots = [0, 1, 4, 2, 5, 3, 6]
    for k in order:
        for slot in slots:
            when(has(slot), lambda: from_c(k, 0, slot).wait_recv())
        out(k, 0).start()
    for slot in slots:
        for k in order:
            if k not in mixed:
                when(has(slot), lambda: from_y(k, slot).wait_recv())
                launch(has(slot), lambda k=k, slot=slot: to_c(k, 1, slot))
    for k in order:
        for slot in slots:
            when(has(slot), lambda: from_c(k, 1, slot).wait_recv())
        out(k, 1).start()
    for ok, copy in waits:
        when(ok, lambda: copy().wait_send())
    lax.fori_loop(1, N, lambda d, _: (tell(d).wait_send(), 0)[1], 0)
    for k in order:
        for side in range(2):
            out(k, side).wait()


def update(g, m, v, w):
    layers = w[0].shape[0]
    count = float(sum(a.size for a in w))
    vmem = pl.BlockSpec(memory_space=pltpu.VMEM)
    hbm = pl.BlockSpec(memory_space=pl.ANY)
    chunks = 3 * layers
    dma = pltpu.SemaphoreType.DMA
    outs = [jax.ShapeDtypeStruct(a.shape, BF16) for a in w] + [jax.ShapeDtypeStruct(a.shape, F32) for a in (*m, *v)]
    return pl.pallas_call(
        functools.partial(update_kernel, count, layers),
        out_shape=outs,
        in_specs=[vmem] * 9 + [hbm] * 3,
        out_specs=[hbm] * 3 + [vmem] * 6,
        scratch_shapes=[pltpu.VMEM(a.shape, BF16) for a in w]
        + [pltpu.VMEM(a.shape, BF16) for a in g]
        + [pltpu.VMEM((N, 8, 128), F32)]
        + [dma((3,)), dma((N,)), dma((N,)), dma((chunks + 1, 2, Z)), dma((chunks + 1, 2, Z)), dma((chunks, 7)), dma((chunks, 7)),
           dma((chunks, 2, 7)), dma((chunks, 2, 7)), dma((chunks, 2))],
        compiler_params=pltpu.CompilerParams(collective_id=1, has_side_effects=True, vmem_limit_bytes=60 * 1024 * 1024),
        name="update",
    )(*g, *m, *v, *w)


TILE = 256


def gradient_kernel(layers, *refs):
    acts, aTs, dgs, dus, dhs = (refs[i * layers : (i + 1) * layers] for i in range(5))
    refs = refs[5 * layers :]
    outs, refs = refs[0:3], refs[3:]
    wide, tall, from_c, wide_y, tall_y, wide_z, tall_z, tall_c = refs[:8]
    left, right, aT, dh, wide_sum, tall_sum = refs[8:14]
    tile_sem, keep_sem, send_c, recv_c, send_y, recv_y, send_z, recv_z = refs[14:]
    me, y, z, c = place()
    partner, across = index(y, z, 1 - c), index(1 - y, z, c)
    above, below = index(y, jnp.minimum(z + 1, Z - 1), c), index(y, jnp.maximum(z - 1, 0), c)

    units = []
    for l in reversed(range(layers)):
        units += [(2, l, l), (0, l, 2 * l), (1, l, 2 * l + 1)]
    tiles = {k: (acts[l].shape[0] if i == 2 else dgs[l].shape[1]) // TILE for k, (i, l, s) in enumerate(units)}

    def tile(k, t, slot):
        i, l, _ = units[k]
        at = pl.ds(pl.multiple_of(t * TILE, TILE), TILE)
        if i == 2:
            return pltpu.make_async_copy(acts[l].at[at, :], left.at[slot], tile_sem.at[slot])
        return pltpu.make_async_copy((dgs, dus)[i][l].at[:, at], right.at[slot], tile_sem.at[slot])

    def keep(k):
        i, l, _ = units[k]
        if i == 2:
            return pltpu.make_async_copy(dhs[l], dh, keep_sem.at[0])
        return pltpu.make_async_copy(aTs[l], aT, keep_sem.at[1])

    def unit(k, start, stop):
        i, l, s = units[k]

        def body(t, _):
            slot = lax.rem(t, 2)

            @pl.when(t + 1 < tiles[k])
            def _():
                tile(k, t + 1, 1 - slot).start()

            tile(k, t, slot).wait()
            at = pl.ds(pl.multiple_of(t * TILE, TILE), TILE)
            if i == 2:
                tall[s, at, :] = jnp.dot(left[slot], dh[...], preferred_element_type=F32).astype(BF16)
            else:
                wide[s, :, at] = jnp.dot(aT[...], right[slot], preferred_element_type=F32).astype(BF16)
            return 0

        lax.fori_loop(start, stop, body, 0)

    def parts(k):
        i, l, s = units[k]
        if i == 2:
            return tall.at[s], tall_c.at[s], tall_y.at[s], tall_z.at[s], tall_sum
        return wide.at[s], from_c.at[s], wide_y.at[s], wide_z.at[s], wide_sum

    def block(k, yy, zz, cc):
        ref = parts(k)[0]
        rows = ref.shape[0] // N
        return ref.at[pl.ds(pl.multiple_of(index(yy, zz, cc) * rows, rows), rows), :]

    def by_rows(rows, f):
        def body(t, _):
            f(pl.ds(pl.multiple_of(t * 16, 16), 16))
            return 0

        lax.fori_loop(0, rows // 16, body, 0)

    def swap(k, half, zz):
        row = 1 - y if half == 0 else y
        return remote(block(k, row, zz, 1 - c), parts(k)[1].at[half, zz], send_c.at[k, half, zz], recv_c.at[k, half, zz], partner)

    def cross(k, zz):
        return remote(block(k, 1 - y, zz, c), parts(k)[2].at[zz], send_y.at[k, zz], recv_y.at[k, zz], across)

    def pass_up(k, zz):
        return remote(block(k, y, zz, c), parts(k)[3].at[zz], send_z.at[k, zz], recv_z.at[k, zz], above)

    def pass_down(k, zz):
        slot = jnp.where(z - 1 == zz, Z, zz)
        return remote(block(k, y, zz, c), parts(k)[3].at[slot], send_z.at[k, zz], recv_z.at[k, slot], below)

    order = [0, 3, 1, 2]

    def step1(k):
        for half in range(2):
            for zz in order:
                swap(k, half, zz).start()

    def step2(k):
        got = parts(k)[1]
        for zz in order:
            swap(k, 0, zz).wait_recv()
            mine = block(k, 1 - y, zz, c)

            def add(at):
                mine[at, :] = (mine[at, :].astype(F32) + got[0, zz, at, :].astype(F32)).astype(BF16)

            by_rows(mine.shape[0], add)
            cross(k, zz).start()

    def step4(k):
        _, got, over, came, total = parts(k)
        i, l, _ = units[k]
        for zz in order:
            swap(k, 1, zz).wait_recv()
            cross(k, zz).wait_recv()
            mine = block(k, y, zz, c)
            rows = mine.shape[0]

            def first(at):
                total[at, :] = mine[at, :].astype(F32) + got[1, zz, at, :].astype(F32) + over[zz, at, :].astype(F32)

            by_rows(rows, first)

            @pl.when((z <= zz) & (z > 0))
            def _():
                pass_up(k, zz).wait_recv()

                def add(at):
                    total[at, :] += came[zz, at, :].astype(F32)

                by_rows(rows, add)

            @pl.when((z >= zz) & (z < Z - 1))
            def _():
                slot = jnp.where(z == zz, Z, zz)
                remote(mine, came.at[slot], send_z.at[k, zz], recv_z.at[k, slot], above).wait_recv()

                def add(at):
                    total[at, :] += came[slot, at, :].astype(F32)

                by_rows(rows, add)

            @pl.when(z == zz)
            def _():
                def store(at):
                    outs[i][l, at, :] = total[at, :].astype(BF16)

                by_rows(rows, store)

            @pl.when(z != zz)
            def _():
                def store(at):
                    mine[at, :] = total[at, :].astype(BF16)

                by_rows(rows, store)

            @pl.when(z < zz)
            def _():
                pass_up(k, zz).start()

            @pl.when(z > zz)
            def _():
                pass_down(k, zz).start()

    tile(0, 0, 0).start()
    keep(0).start()
    keep(1).start()
    barrier = pltpu.get_barrier_semaphore()
    near = [(partner, z >= 0), (across, z >= 0), (above, z < Z - 1), (below, z > 0)]
    for to, ok in near:

        @pl.when(ok)
        def _():
            pl.semaphore_signal(barrier, inc=1, device_id={"dp": to}, device_id_type=MESH)

    for k in range(len(units)):
        if k > 0:
            tile(k, 0, 0).start()
        if units[k][0] == 2 or units[k][0] == 0:
            if k > 1:
                keep(k).start()
            keep(k).wait()
        if k == 0:
            unit(k, 0, tiles[k])
            pl.semaphore_wait(barrier, 2 + (z < Z - 1).astype(jnp.int32) + (z > 0).astype(jnp.int32))
        else:
            unit(k, 0, 3)
            step2(k - 1)
            unit(k, 3, tiles[k])
        step1(k)
        if k == 3:
            step4(0)
    last = len(units) - 1
    step4(1)
    step2(last)
    for k in range(2, len(units)):
        step4(k)
    for k in range(len(units)):
        for zz in range(Z):
            swap(k, 0, zz).wait_send()
            swap(k, 1, zz).wait_send()
            cross(k, zz).wait_send()

            @pl.when(z != zz)
            def _():
                pass_up(k, zz).wait_send()


def gradients(acts, aTs, dgs, dus, dhs):
    layers = len(acts)
    ff, tokens = acts[0].shape
    d = aTs[0].shape[0]
    vmem = pl.BlockSpec(memory_space=pltpu.VMEM)
    hbm = pl.BlockSpec(memory_space=pl.ANY)
    dma = pltpu.SemaphoreType.DMA
    w, t = 2 * layers, layers
    units = 3 * layers
    wr, tr = d // N, ff // N
    return pl.pallas_call(
        functools.partial(gradient_kernel, layers),
        out_shape=[jax.ShapeDtypeStruct(s, BF16) for s in ((layers, wr, ff), (layers, wr, ff), (layers, tr, d))],
        in_specs=[hbm] * (5 * layers),
        out_specs=[vmem] * 3,
        scratch_shapes=[
            pltpu.VMEM((w, d, ff), BF16),
            pltpu.VMEM((t, ff, d), BF16),
            pltpu.VMEM((w, 2, Z, wr, ff), BF16),
            pltpu.VMEM((w, Z, wr, ff), BF16),
            pltpu.VMEM((t, Z, tr, d), BF16),
            pltpu.VMEM((w, Z + 1, wr, ff), BF16),
            pltpu.VMEM((t, Z + 1, tr, d), BF16),
            pltpu.VMEM((t, 2, Z, tr, d), BF16),
            pltpu.VMEM((2, TILE, tokens), BF16),
            pltpu.VMEM((2, tokens, TILE), BF16),
            pltpu.VMEM((d, tokens), BF16),
            pltpu.VMEM((tokens, d), BF16),
            pltpu.VMEM((wr, ff), F32),
            pltpu.VMEM((tr, d), F32),
            dma((2,)),
            dma((2,)),
            dma((units, 2, Z)),
            dma((units, 2, Z)),
            dma((units, Z)),
            dma((units, Z)),
            dma((units, Z)),
            dma((units, Z + 1)),
        ],
        compiler_params=pltpu.CompilerParams(collective_id=2, has_side_effects=True, vmem_limit_bytes=63 * 1024 * 1024),
        name="gradients",
    )(*acts, *aTs, *dgs, *dus, *dhs)


def dot(a, b):
    return jnp.dot(a, b, preferred_element_type=F32)


def dot_t(a, b):
    return lax.dot_general(a, b, (((1,), (1,)), ((), ())), preferred_element_type=F32)


def tokens_kernel(layers, x_ref, dy_ref, wg, wu, wd, *outs):
    actT, aT, dg, du, dh = (outs[i * layers : (i + 1) * layers] for i in range(5))
    saved = []
    h = x_ref[...]
    for l in range(layers):
        wide = h.astype(F32)
        scale = lax.rsqrt(jnp.mean(wide * wide, -1, keepdims=True) + 1e-6)
        a = (wide * scale).astype(BF16)
        aT[l][...] = a.T
        gate, up = dot(a, wg[l]), dot(a, wu[l])
        s = jax.nn.sigmoid(gate)
        silu = gate * s
        act = (silu * up).astype(BF16)
        actT[l][...] = act.T
        saved.append((wide, scale, silu, up * (s + silu * (1.0 - s))))
        if l + 1 < layers:
            h = (h.astype(F32) + dot(act, wd[l]).astype(BF16).astype(F32)).astype(BF16)
    d = dy_ref[...]
    for l in reversed(range(layers)):
        wide, scale, silu, slope = saved[l]
        if l + 1 < layers:
            dh[l][...] = d
        by_act = dot_t(d, wd[l]).astype(BF16).astype(F32)
        by_gate, by_up = (by_act * slope).astype(BF16), (by_act * silu).astype(BF16)
        dg[l][...] = by_gate
        du[l][...] = by_up
        if l > 0:
            by_a = dot_t(by_gate, wg[l]).astype(BF16).astype(F32) + dot_t(by_up, wu[l]).astype(BF16).astype(F32)
            by_a = by_a.astype(BF16).astype(F32)
            pull = jnp.mean(by_a * wide, -1, keepdims=True)
            back = (by_a * scale - wide * (scale * scale * scale * pull)).astype(BF16)
            d = (d.astype(F32) + back.astype(F32)).astype(BF16)


def through(x, dy, wg, wu, wd):
    layers, dm, ff = wg.shape
    tokens = x.shape[0]
    t = 256
    tall, flat = pl.BlockSpec((t, dm), lambda i: (i, 0)), pl.BlockSpec((t, ff), lambda i: (i, 0))
    whole = lambda w: pl.BlockSpec(w.shape, lambda i: (0, 0, 0), pipeline_mode=pl.Buffered(1))
    shape = lambda *s: jax.ShapeDtypeStruct(s, BF16)
    outs = pl.pallas_call(
        functools.partial(tokens_kernel, layers),
        grid=(tokens // t,),
        in_specs=[tall, tall, whole(wg), whole(wu), whole(wd)],
        out_specs=[pl.BlockSpec((ff, t), lambda i: (0, i))] * layers
        + [pl.BlockSpec((dm, t), lambda i: (0, i))] * layers
        + [flat] * (2 * layers)
        + [tall] * (layers - 1),
        out_shape=[shape(ff, tokens)] * layers + [shape(dm, tokens)] * layers + [shape(tokens, ff)] * (2 * layers) + [shape(tokens, dm)] * (layers - 1),
        compiler_params=pltpu.CompilerParams(dimension_semantics=("arbitrary",), vmem_limit_bytes=63 * 1024 * 1024),
        name="tokens",
    )(x, dy, wg, wu, wd)
    return [list(outs[i * layers : (i + 1) * layers]) for i in range(4)] + [[*outs[4 * layers :], dy]]


def solution(mesh):
    def step(x, dy, *arrays):
        w, m, v = (arrays[i : i + 3] for i in (0, 3, 6))
        g = gradients(*through(x[0], dy[0], *w))
        return tuple(update(g, m, v, w))

    opt = P(None, "dp", None)
    return jax.shard_map(
        step,
        mesh=mesh,
        in_specs=(P(("rep", "dp")), P(("rep", "dp")), P(), P(), P(), *[opt] * 6),
        out_specs=(*[P("rep")] * 3, *[P("rep", "dp")] * 6),
        check_vma=False,
    )
```

time: 1150 us -> 497 us (0.43)
  Pallas kernels: 0 us -> 478 us
  waiting for transfers between devices: 327 us -> 0 us
  matrix products: 277 us -> 0 us
  starting transfers between devices: 220 us -> 0 us
  other arithmetic: 154 us -> 0.01 us
  loops' own time: 48.2 us -> 0 us
  local copies, waits for them, and re-layouts: 64.5 us -> 17.8 us
  blocking collectives: 30.6 us -> 0 us
  between operations: 17.8 us -> 0.7 us
    pallas_call x0 -> x3, Pallas kernels: none -> 478 us  [the longest x1 277 us: gradients(): pl.pallas_call(functools.partial(gradient_kernel, layers), out_shape=[jax...]
    dot_general x57 -> x0, matrix products: 277 us -> none  [the longest x19 111 us: layer(): gate = jnp.dot(a, w['w_gate'], preferred_element_type=jnp.float32)]
    dot_general x102 -> x0, starting transfers between devices: 219 us -> none  [the longest x34 75 us: matmul(): jnp.dot(a, w, preferred_element_type=jnp.float32).astype(jnp.bfloat16)]
    reshape x3 -> x0, waiting for transfers between devices: 168 us -> none  [step(): t.reshape(-1, *t.shape[2:])]
    dot_general x102 -> x0, waiting for transfers between devices: 160 us -> none  [the longest x34 68.7 us: matmul(): jnp.dot(a, w, preferred_element_type=jnp.float32).astype(jnp.bfloat16)]
    dot_general x96 -> x0, other arithmetic: 112 us -> none
    another operation x6 -> x0, loops' own time: 48.2 us -> none  [the longest x2 16.7 us: layer(): up = jnp.dot(a, w['w_up'], preferred_element_type=jnp.float32)]
    unnamed x59 -> x27, local copies, waits for them, and re-layouts: 49.3 us -> 17.8 us
  transfers between devices with their start and end apart: 105 -> 0, of which waited for: 60 -> 0; matrix products, arithmetic and copies ran while one was open for 29% -> 0% of each run, Pallas kernels for 0% -> 0%
where the time goes in v1:
time: 497 us; the launch traced here: 496 us
  Pallas kernels  478 us (96%)
  local copies, waits for them, and re-layouts  17.8 us (4%)
    pallas_call x1, Pallas kernels, gradients(): pl.pallas_call(functools.partial(gradient_kernel, layers), out_shape=[jax...  277 us
    pallas_call x1, Pallas kernels, update(): pl.pallas_call(functools.partial(update_kernel, count, layers), out_shape...  124 us
    pallas_call x1, Pallas kernels, through(): pl.pallas_call(functools.partial(tokens_kernel, layers), grid=(tokens //...  76.6 us
    unnamed x27, local copies, waits for them, and re-layouts  17.8 us

profile of v1, /device:TPU:0, one launch (start us, length us, event | category | flops | bytes accessed | tf_op | source)
XLA Modules:
  0.0 496.1 jit_solution(11319128127973760773)
XLA Ops:
  0.6 76.6 %tokens.1 = (bf16[1792,2048]{1,0:T(8,128)(2,1)}, bf16[1792,2048]{1,0:T(8,128)(2,1)}, bf16[768,2048]{1,0:T(8,128)(2,1)}, bf16[768,2048]{1,0:T(8,128)(2,1)}, bf16[...) custom-call(bf16[2048,768]{1,0:T(8,128)(2,1)} %bitcast.6, ...), custom_call_target="tpu_custom_call" | custom-call | tf_op jit(solution)/shard_map/tokens/pallas_call | solution.py:525
  77.2 276.7 %gradients.1 = (bf16[2,48,1792]{2,1,0:T(8,128)(2,1)}, bf16[2,48,1792]{2,1,0:T(8,128)(2,1)}, bf16[2,112,768]{2,1,0:T(8,128)(2,1)}) custom-call(bf16[1792,2048]{1,0:T(8,128)(2,1)} %get-tuple-element.21.refs_0_, bf16[1792,2048]{1,0:T(8,128)(2,1)} %get-tuple-element.22.refs_1_, bf16[768,2048]{1,0:T(8,128)(2,1)} %get-tuple-element.23.refs_2_, ...), custom_call_target="tpu_custom_call" | custom-call | tf_op jit(solution)/shard_map/gradients/pallas_call | solution.py:442
  353.9 124.4 %update.1 = (bf16[2,768,1792]{2,1,0:T(8,128)(2,1)}, bf16[2,768,1792]{2,1,0:T(8,128)(2,1)}, bf16[2,1792,768]{2,1,0:T(8,128)(2,1)}, f32[2,48,1792]{2,1,0:T(8,128)}...) custom-call(bf16[2,48,1792]{2,1,0:T(8,128)(2,1)} %get-tuple-element., ...), custom_call_target="tpu_custom_call" | custom-call | tf_op jit(solution)/shard_map/update/pallas_call | solution.py:215
  478.3 0.0 copy-start
  478.4 0.0 slice-start
  478.4 5.9 %copy.29 = bf16[2,768,1792]{2,1,0:T(8,128)(2,1)} copy(bf16[2,768,1792]{2,1,0:T(8,128)(2,1)} %get-tuple-element.42) | data formatting | bytes 11010048
  484.2 0.0 copy-done
  484.2 2.8 copy.30
  487.0 0.1 slice-done
  487.1 1.1 slice-done.1
  488.2 0.0 copy-start.2
  488.2 2.8 copy.31
  491.0 0.0 copy-done.6
  491.0 0.8 copy.32
  491.9 0.0 copy-done.5
  491.9 0.8 copy.33
  492.7 0.0 copy-done.4
  492.7 0.8 copy.34
  493.6 0.0 copy-done.3
  493.6 0.8 copy.35
  494.4 0.0 copy-done.2
  494.4 0.8 copy.36
  495.3 0.0 copy-done.1
  495.3 0.8 copy.37
  (7 shorter events, 0.0 us)
Async XLA Ops:
  478.3 5.9 %copy-start = (bf16[2,768,1792]{2,1,0:T(8,128)(2,1)S(1)}, bf16[2,768,1792]{2,1,0:T(8,128)(2,1)}, u32[]{:S(2)}) copy-start(bf16[2,768,1792]{2,1,0:T(8,128)(2,1)} %get-tuple-element.43) | copy-start | bytes 16515076
  478.4 8.7 %slice-start = ((s8[5505024]{0:T(1024)(128)(4,1)}), s8[4194304]{0:T(1024)(128)(4,1)S(1)}, s32[]{:S(2)}) async-start(s8[5505024]{0:T(1024)(128)(4,1)} %bitcast.4), calls=%async_computation | async-start | bytes 8388608
  484.2 4.0 slice-start.1
  488.2 2.8 copy-start.6
  488.2 3.7 copy-start.5
  488.2 4.5 copy-start.4
  488.2 5.4 %copy-start.3 = (f32[2,48,1792]{2,1,0:T(8,128)S(1)}, f32[2,48,1792]{2,1,0:T(8,128)}, u32[]{:S(2)}) copy-start(f32[2,48,1792]{2,1,0:T(8,128)} %get-tuple-element.48) | copy-start | bytes 2064388
  488.2 6.2 %copy-start.2 = (f32[2,48,1792]{2,1,0:T(8,128)S(1)}, f32[2,48,1792]{2,1,0:T(8,128)}, u32[]{:S(2)}) copy-start(f32[2,48,1792]{2,1,0:T(8,128)} %get-tuple-element.49) | copy-start | bytes 2064388
  491.0 4.3 copy-start.1

commit v2 on v1

--- a/solution.py
+++ b/solution.py
@@ -30,9 +30,9 @@
 
 def update_kernel(count, layers, *refs):
     g, m, v, wf = refs[0:3], refs[3:6], refs[6:9], refs[9:12]
-    w_out, m_out, v_out = refs[12:15], refs[15:18], refs[18:21]
-    full, own, norms = refs[21:24], refs[24:27], refs[27]
-    in_sem, norm_send, norm_recv, send_z, recv_z, send_y, recv_y, send_c, recv_c, out_sem = refs[28:]
+    full, m_out, v_out = refs[12:15], refs[15:18], refs[18:21]
+    own, norms = refs[21:24], refs[24]
+    in_sem, norm_send, norm_recv, send_z, recv_z, send_y, recv_y, send_c, recv_c = refs[25:]
     me, y, z, c = place()
     rows = [ref.shape[1] for ref in g]
     loads = []
@@ -177,16 +177,10 @@
                 when(has(slot), lambda: arrived(n, slot).wait_recv())
                 spread(n, slot)
 
-    def out(k, side):
-        i, l = chunks[k]
-        half = pl.ds((y if side == 0 else 1 - y) * (Z * C * rows[i]), Z * C * rows[i])
-        return pltpu.make_async_copy(full[i].at[l, half], w_out[i].at[l, half], out_sem.at[k, side])
-
     slots = [0, 1, 4, 2, 5, 3, 6]
     for k in order:
         for slot in slots:
             when(has(slot), lambda: from_c(k, 0, slot).wait_recv())
-        out(k, 0).start()
     for slot in slots:
         for k in order:
             if k not in mixed:
@@ -195,13 +189,9 @@
     for k in order:
         for slot in slots:
             when(has(slot), lambda: from_c(k, 1, slot).wait_recv())
-        out(k, 1).start()
     for ok, copy in waits:
         when(ok, lambda: copy().wait_send())
     lax.fori_loop(1, N, lambda d, _: (tell(d).wait_send(), 0)[1], 0)
-    for k in order:
-        for side in range(2):
-            out(k, side).wait()
 
 
 def update(g, m, v, w):
@@ -211,18 +201,17 @@
     hbm = pl.BlockSpec(memory_space=pl.ANY)
     chunks = 3 * layers
     dma = pltpu.SemaphoreType.DMA
-    outs = [jax.ShapeDtypeStruct(a.shape, BF16) for a in w] + [jax.ShapeDtypeStruct(a.shape, F32) for a in (*m, *v)]
+    outs = [pltpu.VMEM(a.shape, BF16) for a in w] + [jax.ShapeDtypeStruct(a.shape, F32) for a in (*m, *v)]
     return pl.pallas_call(
         functools.partial(update_kernel, count, layers),
         out_shape=outs,
         in_specs=[vmem] * 9 + [hbm] * 3,
-        out_specs=[hbm] * 3 + [vmem] * 6,
-        scratch_shapes=[pltpu.VMEM(a.shape, BF16) for a in w]
-        + [pltpu.VMEM(a.shape, BF16) for a in g]
+        out_specs=[vmem] * 9,
+        scratch_shapes=[pltpu.VMEM(a.shape, BF16) for a in g]
         + [pltpu.VMEM((N, 8, 128), F32)]
         + [dma((3,)), dma((N,)), dma((N,)), dma((chunks + 1, 2, Z)), dma((chunks + 1, 2, Z)), dma((chunks, 7)), dma((chunks, 7)),
-           dma((chunks, 2, 7)), dma((chunks, 2, 7)), dma((chunks, 2))],
-        compiler_params=pltpu.CompilerParams(collective_id=1, has_side_effects=True, vmem_limit_bytes=60 * 1024 * 1024),
+           dma((chunks, 2, 7)), dma((chunks, 2, 7))],
+        compiler_params=pltpu.CompilerParams(collective_id=1, has_side_effects=True, vmem_limit_bytes=36 * 1024 * 1024),
         name="update",
     )(*g, *m, *v, *w)
 
@@ -297,93 +286,94 @@
 
         lax.fori_loop(0, rows // 16, body, 0)
 
-    def swap(k, half, zz):
+    end = (z == 0) | (z == Z - 1)
+
+    def piece(n):
+        far = (jnp.where(z < 2, Z - 1, 0), jnp.where(end, jnp.where(z == 0, 2, 1), jnp.where(z == 1, 0, Z - 1)), jnp.where(end, Z - 2 - jnp.where(z == 0, 1, 0), 3 - z), z)
+        return far[n]
+
+    def swap(k, half, n):
+        zz = piece(n)
         row = 1 - y if half == 0 else y
-        return remote(block(k, row, zz, 1 - c), parts(k)[1].at[half, zz], send_c.at[k, half, zz], recv_c.at[k, half, zz], partner)
-
-    def cross(k, zz):
-        return remote(block(k, 1 - y, zz, c), parts(k)[2].at[zz], send_y.at[k, zz], recv_y.at[k, zz], across)
-
-    def pass_up(k, zz):
-        return remote(block(k, y, zz, c), parts(k)[3].at[zz], send_z.at[k, zz], recv_z.at[k, zz], above)
-
-    def pass_down(k, zz):
+        return remote(block(k, row, zz, 1 - c), parts(k)[1].at[half, zz], send_c.at[k, half, n], recv_c.at[k, half, n], partner)
+
+    def cross(k, n):
+        zz = piece(n)
+        return remote(block(k, 1 - y, zz, c), parts(k)[2].at[zz], send_y.at[k, n], recv_y.at[k, n], across)
+
+    def pass_on(k, n):
+        zz = piece(n)
         slot = jnp.where(z - 1 == zz, Z, zz)
-        return remote(block(k, y, zz, c), parts(k)[3].at[slot], send_z.at[k, zz], recv_z.at[k, slot], below)
-
-    order = [0, 3, 1, 2]
+        return remote(block(k, y, zz, c), parts(k)[3].at[slot], send_z.at[k, n], recv_z.at[k, slot], jnp.where(zz > z, above, below))
+
+    def passed(k, slot):
+        ref = parts(k)[3].at[slot]
+        return remote(ref, ref, send_z.at[k, 0], recv_z.at[k, slot], jnp.where(end, jnp.where(z == 0, above, below), above))
 
     def step1(k):
         for half in range(2):
-            for zz in order:
-                swap(k, half, zz).start()
+            for n in range(Z):
+                swap(k, half, n).start()
 
     def step2(k):
         got = parts(k)[1]
-        for zz in order:
-            swap(k, 0, zz).wait_recv()
+        for n in range(Z):
+            zz = piece(n)
+            swap(k, 0, n).wait_recv()
             mine = block(k, 1 - y, zz, c)
 
             def add(at):
                 mine[at, :] = (mine[at, :].astype(F32) + got[0, zz, at, :].astype(F32)).astype(BF16)
 
             by_rows(mine.shape[0], add)
-            cross(k, zz).start()
+            cross(k, n).start()
+
+    def gather(k, n):
+        _, got, over, _, total = parts(k)
+        zz = piece(n)
+        swap(k, 1, n).wait_recv()
+        cross(k, n).wait_recv()
+        mine = block(k, y, zz, c)
+
+        def first(at):
+            total[at, :] = mine[at, :].astype(F32) + got[1, zz, at, :].astype(F32) + over[zz, at, :].astype(F32)
+
+        by_rows(mine.shape[0], first)
+        return mine, total
+
+    def also(k, ok, slot):
+        _, _, _, came, total = parts(k)
+
+        @pl.when(ok)
+        def _():
+            passed(k, slot).wait_recv()
+
+            def add(at):
+                total[at, :] += came[slot, at, :].astype(F32)
+
+            by_rows(total.shape[0], add)
+
+    def step3(k):
+        for n in range(Z - 1):
+            mine, total = gather(k, n)
+            also(k, jnp.logical_not(end), piece(n))
+
+            def store(at):
+                mine[at, :] = total[at, :].astype(BF16)
+
+            by_rows(mine.shape[0], store)
+            pass_on(k, n).start()
 
     def step4(k):
-        _, got, over, came, total = parts(k)
         i, l, _ = units[k]
-        for zz in order:
-            swap(k, 1, zz).wait_recv()
-            cross(k, zz).wait_recv()
-            mine = block(k, y, zz, c)
-            rows = mine.shape[0]
-
-            def first(at):
-                total[at, :] = mine[at, :].astype(F32) + got[1, zz, at, :].astype(F32) + over[zz, at, :].astype(F32)
-
-            by_rows(rows, first)
-
-            @pl.when((z <= zz) & (z > 0))
-            def _():
-                pass_up(k, zz).wait_recv()
-
-                def add(at):
-                    total[at, :] += came[zz, at, :].astype(F32)
-
-                by_rows(rows, add)
-
-            @pl.when((z >= zz) & (z < Z - 1))
-            def _():
-                slot = jnp.where(z == zz, Z, zz)
-                remote(mine, came.at[slot], send_z.at[k, zz], recv_z.at[k, slot], above).wait_recv()
-
-                def add(at):
-                    total[at, :] += came[slot, at, :].astype(F32)
-
-                by_rows(rows, add)
-
-            @pl.when(z == zz)
-            def _():
-                def store(at):
-                    outs[i][l, at, :] = total[at, :].astype(BF16)
-
-                by_rows(rows, store)
-
-            @pl.when(z != zz)
-            def _():
-                def store(at):
-                    mine[at, :] = total[at, :].astype(BF16)
-
-                by_rows(rows, store)
-
-            @pl.when(z < zz)
-            def _():
-                pass_up(k, zz).start()
-
-            @pl.when(z > zz)
-            def _():
-                pass_down(k, zz).start()
+        mine, total = gather(k, Z - 1)
+        also(k, z > 0, z)
+        also(k, z < Z - 1, Z)
+
+        def store(at):
+            outs[i][l, at, :] = total[at, :].astype(BF16)
+
+        by_rows(mine.shape[0], store)
 
     tile(0, 0, 0).start()
     keep(0).start()
@@ -411,22 +401,22 @@
             step2(k - 1)
             unit(k, 3, tiles[k])
         step1(k)
-        if k == 3:
-            step4(0)
+        if k in (3, 4):
+            step3(k - 3)
     last = len(units) - 1
-    step4(1)
     step2(last)
     for k in range(2, len(units)):
-        step4(k)
+        step3(k)
+        step4(k - 2)
+    step4(last - 1)
+    step4(last)
     for k in range(len(units)):
-        for zz in range(Z):
-            swap(k, 0, zz).wait_send()
-            swap(k, 1, zz).wait_send()
-            cross(k, zz).wait_send()
-
-            @pl.when(z != zz)
-            def _():
-                pass_up(k, zz).wait_send()
+        for n in range(Z):
+            swap(k, 0, n).wait_send()
+            swap(k, 1, n).wait_send()
+            cross(k, n).wait_send()
+            if n < Z - 1:
+                pass_on(k, n).wait_send()
 
 
 def gradients(acts, aTs, dgs, dus, dhs):
@@ -441,7 +431,7 @@
     wr, tr = d // N, ff // N
     return pl.pallas_call(
         functools.partial(gradient_kernel, layers),
-        out_shape=[jax.ShapeDtypeStruct(s, BF16) for s in ((layers, wr, ff), (layers, wr, ff), (layers, tr, d))],
+        out_shape=[pltpu.VMEM(s, BF16) for s in ((layers, wr, ff), (layers, wr, ff), (layers, tr, d))],
         in_specs=[hbm] * (5 * layers),
         out_specs=[vmem] * 3,
         scratch_shapes=[
@@ -468,7 +458,7 @@
             dma((units, Z)),
             dma((units, Z + 1)),
         ],
-        compiler_params=pltpu.CompilerParams(collective_id=2, has_side_effects=True, vmem_limit_bytes=63 * 1024 * 1024),
+        compiler_params=pltpu.CompilerParams(collective_id=2, has_side_effects=True, vmem_limit_bytes=60 * 1024 * 1024),
         name="gradients",
     )(*acts, *aTs, *dgs, *dus, *dhs)
 

time: 497 us -> 313 us (0.63)
  Pallas kernels: 478 us -> 299 us
  local copies, waits for them, and re-layouts: 17.8 us -> 12.8 us
    pallas_call x1, Pallas kernels: 277 us -> 120 us  [gradients(): pl.pallas_call(functools.partial(gradient_kernel, layers), out_shape=[plt...]
    pallas_call x1, Pallas kernels: 124 us -> 102 us  [update(): pl.pallas_call(functools.partial(update_kernel, count, layers), out_shape...]
    unnamed x27 -> x19, local copies, waits for them, and re-layouts: 17.8 us -> 12.8 us
where the time goes in v2:
time: 313 us; the launch traced here: 312 us
  Pallas kernels  299 us (96%)
  local copies, waits for them, and re-layouts  12.8 us (4%)
    pallas_call x1, Pallas kernels, gradients(): pl.pallas_call(functools.partial(gradient_kernel, layers), out_shape=[plt...  120 us
    pallas_call x1, Pallas kernels, update(): pl.pallas_call(functools.partial(update_kernel, count, layers), out_shape...  102 us
    pallas_call x1, Pallas kernels, through(): pl.pallas_call(functools.partial(tokens_kernel, layers), grid=(tokens //...  76.6 us
    unnamed x19, local copies, waits for them, and re-layouts  12.8 us

profile of v2, /device:TPU:0, one launch (start us, length us, event | category | flops | bytes accessed | tf_op | source)
XLA Modules:
  0.0 312.0 jit_solution(8784874176222349804)
XLA Ops:
  0.6 76.6 %tokens.1 = (bf16[1792,2048]{1,0:T(8,128)(2,1)}, bf16[1792,2048]{1,0:T(8,128)(2,1)}, bf16[768,2048]{1,0:T(8,128)(2,1)}, bf16[768,2048]{1,0:T(8,128)(2,1)}, bf16[...) custom-call(bf16[2048,768]{1,0:T(8,128)(2,1)} %bitcast.4, ...), custom_call_target="tpu_custom_call" | custom-call | tf_op jit(solution)/shard_map/tokens/pallas_call | solution.py:515
  77.2 120.0 %gradients.1 = (bf16[2,48,1792]{2,1,0:T(8,128)(2,1)S(1)}, bf16[2,48,1792]{2,1,0:T(8,128)(2,1)S(1)}, bf16[2,112,768]{2,1,0:T(8,128)(2,1)S(1)}) custom-call(bf16[1792,2048]{1,0:T(8,128)(2,1)} %get-tuple-element.21.refs_0_, bf16[1792,2048]{1,0:T(8,128)(2,1)} %get-tuple-element.22.refs_1_, bf16[768,2048]{1,0:T(8,128)(2,1)} %get-tuple-element.23.refs_2_, ...), custom_call_target="tpu_custom_call" | custom-call | tf_op jit(solution)/shard_map/gradients/pallas_call | solution.py:432
  197.2 102.0 %update.1 = (bf16[2,768,1792]{2,1,0:T(8,128)(2,1)S(1)}, bf16[2,768,1792]{2,1,0:T(8,128)(2,1)S(1)}, bf16[2,1792,768]{2,1,0:T(8,128)(2,1)S(1)}, f32[2,48,1792]{2,1...) custom-call(bf16[2,48,1792]{2,1,0:T(8,128)(2,1)S(1)} %get-tuple-elem, ...), custom_call_target="tpu_custom_call" | custom-call | tf_op jit(solution)/shard_map/update/pallas_call | solution.py:205
  299.2 2.4 copy.29
  301.6 2.4 copy.30
  304.1 0.0 copy-start.4
  304.1 0.0 copy-start.3
  304.1 0.0 copy-start.2
  304.1 0.0 copy-start.1
  304.1 2.8 copy.31
  306.9 0.0 copy-start
  306.9 0.8 copy.32
  307.7 0.0 copy-done.4
  307.7 0.8 copy.33
  308.6 0.0 copy-done.3
  308.6 0.8 copy.34
  309.4 0.0 copy-done.2
  309.5 0.8 copy.35
  310.3 0.0 copy-done.1
  310.3 0.8 copy.36
  311.1 0.0 copy-done
  311.2 0.8 copy.37
Async XLA Ops:
  304.1 3.7 %copy-start.4 = (f32[2,48,1792]{2,1,0:T(8,128)S(1)}, f32[2,48,1792]{2,1,0:T(8,128)}, u32[]{:S(2)}) copy-start(f32[2,48,1792]{2,1,0:T(8,128)} %get-tuple-element.55) | copy-start | bytes 2064388
  304.1 4.5 %copy-start.3 = (f32[2,112,768]{2,1,0:T(8,128)S(1)}, f32[2,112,768]{2,1,0:T(8,128)}, u32[]{:S(2)}) copy-start(f32[2,112,768]{2,1,0:T(8,128)} %get-tuple-element.56) | copy-start | bytes 2064388
  304.1 5.4 %copy-start.2 = (f32[2,48,1792]{2,1,0:T(8,128)S(1)}, f32[2,48,1792]{2,1,0:T(8,128)}, u32[]{:S(2)}) copy-start(f32[2,48,1792]{2,1,0:T(8,128)} %get-tuple-element.57) | copy-start | bytes 2064388
  304.1 6.2 %copy-start.1 = (f32[2,48,1792]{2,1,0:T(8,128)S(1)}, f32[2,48,1792]{2,1,0:T(8,128)}, u32[]{:S(2)}) copy-start(f32[2,48,1792]{2,1,0:T(8,128)} %get-tuple-element.58) | copy-start | bytes 2064388
  306.9 4.3 %copy-start = (f32[2,112,768]{2,1,0:T(8,128)S(1)}, f32[2,112,768]{2,1,0:T(8,128)}, u32[]{:S(2)}) copy-start(f32[2,112,768]{2,1,0:T(8,128)} %get-tuple-element.59) | copy-start | bytes 2064388

commit v3 on v2

--- a/solution.py
+++ b/solution.py
@@ -83,8 +83,73 @@
     chunks = [(i, l) for l in range(layers) for i in range(3)]
     mixed = {len(chunks) - 1}
 
-    for i, l in chunks:
-
+    def block(k, yy, zz, cc):
+        i, l = chunks[k]
+        return full[i].at[l, pl.ds(index(yy, zz, cc) * rows[i], rows[i])]
+
+    def origin(slot):
+        return z - slot if slot < 4 else z + slot - 3
+
+    def has(slot):
+        if slot == 0:
+            return z >= 0
+        return z >= slot if slot < 4 else z + slot - 3 < Z
+
+    def to_y(k, slot):
+        ref = block(k, y, origin(slot), c)
+        return remote(ref, ref, send_y.at[k, slot], recv_y.at[k, slot], index(1 - y, z, c))
+
+    def from_y(k, slot):
+        ref = block(k, 1 - y, origin(slot), c)
+        return remote(ref, ref, send_y.at[k, slot], recv_y.at[k, slot], index(1 - y, z, c))
+
+    def to_c(k, side, slot):
+        ref = block(k, y if side == 0 else 1 - y, origin(slot), c)
+        return remote(ref, ref, send_c.at[k, side, slot], recv_c.at[k, side, slot], index(y, z, 1 - c))
+
+    def from_c(k, side, slot):
+        ref = block(k, y if side == 0 else 1 - y, origin(slot), 1 - c)
+        return remote(ref, ref, send_c.at[k, side, slot], recv_c.at[k, side, slot], index(y, z, 1 - c))
+
+    lanes = [(k, 0) for k in range(len(chunks))] + [(k, 1) for k in sorted(mixed)]
+
+    def line(n, slot, up):
+        k, side = lanes[n]
+        ref = block(k, y if side == 0 else 1 - y, origin(slot), c)
+        hop = (slot if slot else 0) if up else (slot - 3 if slot else 0)
+        return remote(ref, ref, send_z.at[n, 0 if up else 1, hop], recv_z.at[n, 0 if up else 1, hop],
+                      index(y, jnp.minimum(z + 1, Z - 1) if up else jnp.maximum(z - 1, 0), c))
+
+    def arrived(n, slot):
+        k, side = lanes[n]
+        up = slot < 4
+        ref = block(k, y if side == 0 else 1 - y, origin(slot), c)
+        hop = slot - 1 if up else slot - 4
+        return remote(ref, ref, send_z.at[n, 0 if up else 1, hop], recv_z.at[n, 0 if up else 1, hop],
+                      index(y, jnp.maximum(z - 1, 0) if up else jnp.minimum(z + 1, Z - 1), c))
+
+    def when(ok, f):
+        pl.when(ok)(f)
+
+    waits = []
+
+    def launch(ok, copy):
+        when(ok, lambda: copy().start())
+        waits.append((ok, copy))
+
+    def spread(n, slot):
+        k, side = lanes[n]
+        ok = has(slot)
+        if slot < 4:
+            launch(ok & (z < Z - 1), lambda: line(n, slot, True))
+        if slot == 0 or slot >= 4:
+            launch(ok & (z > 0), lambda: line(n, slot, False))
+        if side == 0 and (k not in mixed or slot == 0):
+            launch(ok, lambda: to_y(k, slot))
+        launch(ok, lambda: to_c(k, side, slot))
+
+    order = sorted(range(len(chunks)), key=lambda k: k not in mixed)
+    def renew(i, l):
         def adamw(t, _):
             at = pl.ds(pl.multiple_of(t * 16, 16), 16)
             grad = g[i][l, at, :].astype(F32) * factor
@@ -99,78 +164,13 @@
 
         lax.fori_loop(0, rows[i] // 16, adamw, 0)
 
-    def block(k, yy, zz, cc):
-        i, l = chunks[k]
-        return full[i].at[l, pl.ds(index(yy, zz, cc) * rows[i], rows[i])]
-
-    def origin(slot):
-        return z - slot if slot < 4 else z + slot - 3
-
-    def has(slot):
-        if slot == 0:
-            return z >= 0
-        return z >= slot if slot < 4 else z + slot - 3 < Z
-
-    def to_y(k, slot):
-        ref = block(k, y, origin(slot), c)
-        return remote(ref, ref, send_y.at[k, slot], recv_y.at[k, slot], index(1 - y, z, c))
-
-    def from_y(k, slot):
-        ref = block(k, 1 - y, origin(slot), c)
-        return remote(ref, ref, send_y.at[k, slot], recv_y.at[k, slot], index(1 - y, z, c))
-
-    def to_c(k, side, slot):
-        ref = block(k, y if side == 0 else 1 - y, origin(slot), c)
-        return remote(ref, ref, send_c.at[k, side, slot], recv_c.at[k, side, slot], index(y, z, 1 - c))
-
-    def from_c(k, side, slot):
-        ref = block(k, y if side == 0 else 1 - y, origin(slot), 1 - c)
-        return remote(ref, ref, send_c.at[k, side, slot], recv_c.at[k, side, slot], index(y, z, 1 - c))
-
-    lanes = [(k, 0) for k in range(len(chunks))] + [(k, 1) for k in sorted(mixed)]
-
-    def line(n, slot, up):
-        k, side = lanes[n]
-        ref = block(k, y if side == 0 else 1 - y, origin(slot), c)
-        hop = (slot if slot else 0) if up else (slot - 3 if slot else 0)
-        return remote(ref, ref, send_z.at[n, 0 if up else 1, hop], recv_z.at[n, 0 if up else 1, hop],
-                      index(y, jnp.minimum(z + 1, Z - 1) if up else jnp.maximum(z - 1, 0), c))
-
-    def arrived(n, slot):
-        k, side = lanes[n]
-        up = slot < 4
-        ref = block(k, y if side == 0 else 1 - y, origin(slot), c)
-        hop = slot - 1 if up else slot - 4
-        return remote(ref, ref, send_z.at[n, 0 if up else 1, hop], recv_z.at[n, 0 if up else 1, hop],
-                      index(y, jnp.maximum(z - 1, 0) if up else jnp.minimum(z + 1, Z - 1), c))
-
-    def when(ok, f):
-        pl.when(ok)(f)
-
-    waits = []
-
-    def launch(ok, copy):
-        when(ok, lambda: copy().start())
-        waits.append((ok, copy))
-
-    def spread(n, slot):
-        k, side = lanes[n]
-        ok = has(slot)
-        if slot < 4:
-            launch(ok & (z < Z - 1), lambda: line(n, slot, True))
-        if slot == 0 or slot >= 4:
-            launch(ok & (z > 0), lambda: line(n, slot, False))
-        if side == 0 and (k not in mixed or slot == 0):
-            launch(ok, lambda: to_y(k, slot))
-        launch(ok, lambda: to_c(k, side, slot))
-
-    order = sorted(range(len(chunks)), key=lambda k: k not in mixed)
     for k in order:
+        renew(*chunks[k])
         spread(k, 0)
     for k in sorted(mixed):
         from_y(k, 0).wait_recv()
         spread(lanes.index((k, 1)), 0)
-    ranked = sorted(range(len(lanes)), key=lambda n: lanes[n][0] not in mixed)
+    ranked = sorted(range(len(lanes)), key=lambda n: lanes[n][0] in mixed)
     for hop in range(1, Z):
         for n in ranked:
             for slot in (hop, hop + 3):
@@ -233,13 +233,17 @@
     units = []
     for l in reversed(range(layers)):
         units += [(2, l, l), (0, l, 2 * l), (1, l, 2 * l + 1)]
-    tiles = {k: (acts[l].shape[0] if i == 2 else dgs[l].shape[1]) // TILE for k, (i, l, s) in enumerate(units)}
+    tiles = [2 * Z if i == 2 else dgs[l].shape[1] // TILE for i, l, _ in units]
+    tall_tile = acts[0].shape[0] // (2 * Z)
+
+    def rows_of(t):
+        return pl.ds(pl.multiple_of(lax.rem(t + Z * (1 - y), 2 * Z) * tall_tile, tall_tile), tall_tile)
 
     def tile(k, t, slot):
         i, l, _ = units[k]
+        if i == 2:
+            return pltpu.make_async_copy(acts[l].at[rows_of(t), :], left.at[slot], tile_sem.at[slot])
         at = pl.ds(pl.multiple_of(t * TILE, TILE), TILE)
-        if i == 2:
-            return pltpu.make_async_copy(acts[l].at[at, :], left.at[slot], tile_sem.at[slot])
         return pltpu.make_async_copy((dgs, dus)[i][l].at[:, at], right.at[slot], tile_sem.at[slot])
 
     def keep(k):
@@ -261,7 +265,7 @@
             tile(k, t, slot).wait()
             at = pl.ds(pl.multiple_of(t * TILE, TILE), TILE)
             if i == 2:
-                tall[s, at, :] = jnp.dot(left[slot], dh[...], preferred_element_type=F32).astype(BF16)
+                tall[s, rows_of(t), :] = jnp.dot(left[slot], dh[...], preferred_element_type=F32).astype(BF16)
             else:
                 wide[s, :, at] = jnp.dot(aT[...], right[slot], preferred_element_type=F32).astype(BF16)
             return 0
@@ -310,10 +314,9 @@
         ref = parts(k)[3].at[slot]
         return remote(ref, ref, send_z.at[k, 0], recv_z.at[k, slot], jnp.where(end, jnp.where(z == 0, above, below), above))
 
-    def step1(k):
-        for half in range(2):
-            for n in range(Z):
-                swap(k, half, n).start()
+    def step1(k, half):
+        for n in range(Z):
+            swap(k, half, n).start()
 
     def step2(k):
         got = parts(k)[1]
@@ -394,13 +397,23 @@
                 keep(k).start()
             keep(k).wait()
         if k == 0:
+            unit(k, 0, Z)
+            pl.semaphore_wait(barrier, 2 + (z < Z - 1).astype(jnp.int32) + (z > 0).astype(jnp.int32))
+            step1(k, 0)
+            unit(k, Z, Z + 2)
+            step2(k)
+            unit(k, Z + 2, tiles[k])
+            step1(k, 1)
+        elif k == 1:
             unit(k, 0, tiles[k])
-            pl.semaphore_wait(barrier, 2 + (z < Z - 1).astype(jnp.int32) + (z > 0).astype(jnp.int32))
+            step1(k, 0)
+            step1(k, 1)
         else:
             unit(k, 0, 3)
             step2(k - 1)
             unit(k, 3, tiles[k])
-        step1(k)
+            step1(k, 0)
+            step1(k, 1)
         if k in (3, 4):
             step3(k - 3)
     last = len(units) - 1
@@ -443,7 +456,7 @@
             pltpu.VMEM((w, Z + 1, wr, ff), BF16),
             pltpu.VMEM((t, Z + 1, tr, d), BF16),
             pltpu.VMEM((t, 2, Z, tr, d), BF16),
-            pltpu.VMEM((2, TILE, tokens), BF16),
+            pltpu.VMEM((2, ff // (2 * Z), tokens), BF16),
             pltpu.VMEM((2, tokens, TILE), BF16),
             pltpu.VMEM((d, tokens), BF16),
             pltpu.VMEM((tokens, d), BF16),
@@ -471,34 +484,67 @@
     return lax.dot_general(a, b, (((1,), (1,)), ((), ())), preferred_element_type=F32)
 
 
-def tokens_kernel(layers, x_ref, dy_ref, wg, wu, wd, *outs):
-    actT, aT, dg, du, dh = (outs[i * layers : (i + 1) * layers] for i in range(5))
+CHUNK = 256
+
+
+def tokens_kernel(layers, x_ref, dy_ref, *refs):
+    given, refs = refs[0:3], refs[3:]
+    actT, aT, dg, du = (refs[i * layers : (i + 1) * layers] for i in range(4))
+    refs = refs[4 * layers :]
+    dh, refs = refs[: layers - 1], refs[layers - 1 :]
+    wg, wu, wd, act, silu, slope, sem = refs
+    ff = wg.shape[2]
+    first = pl.program_id(0) == 0
+    held = (wg, wu, wd)
+
+    def load(i, l):
+        return pltpu.make_async_copy(given[i].at[l], held[i].at[l], sem.at[i, l])
+
+    @pl.when(first)
+    def _():
+        for l in range(layers):
+            for i in range(3):
+                load(i, l).start()
+
+    def ready(l):
+        @pl.when(first)
+        def _():
+            for i in range(3):
+                load(i, l).wait()
+
     saved = []
     h = x_ref[...]
     for l in range(layers):
         wide = h.astype(F32)
         scale = lax.rsqrt(jnp.mean(wide * wide, -1, keepdims=True) + 1e-6)
         a = (wide * scale).astype(BF16)
+        saved.append((wide, scale))
+        ready(l)
         aT[l][...] = a.T
-        gate, up = dot(a, wg[l]), dot(a, wu[l])
-        s = jax.nn.sigmoid(gate)
-        silu = gate * s
-        act = (silu * up).astype(BF16)
-        actT[l][...] = act.T
-        saved.append((wide, scale, silu, up * (s + silu * (1.0 - s))))
+        for f in range(0, ff, CHUNK):
+            at = slice(f, f + CHUNK)
+            gate, up = dot(a, wg[l, :, at]), dot(a, wu[l, :, at])
+            s = jax.nn.sigmoid(gate)
+            mine = gate * s
+            now = (mine * up).astype(BF16)
+            act[:, at] = now
+            actT[l][at, :] = now.T
+            silu[l, :, at] = mine
+            slope[l, :, at] = up * (s + mine * (1.0 - s))
         if l + 1 < layers:
-            h = (h.astype(F32) + dot(act, wd[l]).astype(BF16).astype(F32)).astype(BF16)
+            h = (h.astype(F32) + dot(act[...], wd[l]).astype(BF16).astype(F32)).astype(BF16)
     d = dy_ref[...]
     for l in reversed(range(layers)):
-        wide, scale, silu, slope = saved[l]
+        wide, scale = saved[l]
         if l + 1 < layers:
             dh[l][...] = d
-        by_act = dot_t(d, wd[l]).astype(BF16).astype(F32)
-        by_gate, by_up = (by_act * slope).astype(BF16), (by_act * silu).astype(BF16)
-        dg[l][...] = by_gate
-        du[l][...] = by_up
+        for f in range(0, ff, CHUNK):
+            at = slice(f, f + CHUNK)
+            by_act = dot_t(d, wd[l, at, :]).astype(BF16).astype(F32)
+            dg[l][:, at] = (by_act * slope[l, :, at]).astype(BF16)
+            du[l][:, at] = (by_act * silu[l, :, at]).astype(BF16)
         if l > 0:
-            by_a = dot_t(by_gate, wg[l]).astype(BF16).astype(F32) + dot_t(by_up, wu[l]).astype(BF16).astype(F32)
+            by_a = dot_t(dg[l][...], wg[l]).astype(BF16).astype(F32) + dot_t(du[l][...], wu[l]).astype(BF16).astype(F32)
             by_a = by_a.astype(BF16).astype(F32)
             pull = jnp.mean(by_a * wide, -1, keepdims=True)
             back = (by_a * scale - wide * (scale * scale * scale * pull)).astype(BF16)
@@ -510,17 +556,19 @@
     tokens = x.shape[0]
     t = 256
     tall, flat = pl.BlockSpec((t, dm), lambda i: (i, 0)), pl.BlockSpec((t, ff), lambda i: (i, 0))
-    whole = lambda w: pl.BlockSpec(w.shape, lambda i: (0, 0, 0), pipeline_mode=pl.Buffered(1))
+    hbm = pl.BlockSpec(memory_space=pl.ANY)
     shape = lambda *s: jax.ShapeDtypeStruct(s, BF16)
     outs = pl.pallas_call(
         functools.partial(tokens_kernel, layers),
         grid=(tokens // t,),
-        in_specs=[tall, tall, whole(wg), whole(wu), whole(wd)],
+        in_specs=[tall, tall, hbm, hbm, hbm],
         out_specs=[pl.BlockSpec((ff, t), lambda i: (0, i))] * layers
         + [pl.BlockSpec((dm, t), lambda i: (0, i))] * layers
         + [flat] * (2 * layers)
         + [tall] * (layers - 1),
         out_shape=[shape(ff, tokens)] * layers + [shape(dm, tokens)] * layers + [shape(tokens, ff)] * (2 * layers) + [shape(tokens, dm)] * (layers - 1),
+        scratch_shapes=[pltpu.VMEM(a.shape, BF16) for a in (wg, wu, wd)]
+        + [pltpu.VMEM((t, ff), BF16), pltpu.VMEM((layers, t, ff), F32), pltpu.VMEM((layers, t, ff), F32), pltpu.SemaphoreType.DMA((3, layers))],
         compiler_params=pltpu.CompilerParams(dimension_semantics=("arbitrary",), vmem_limit_bytes=63 * 1024 * 1024),
         name="tokens",
     )(x, dy, wg, wu, wd)

time: 313 us -> 308 us (0.984)
  Pallas kernels: 299 us -> 294 us
    pallas_call x1, Pallas kernels: 76.6 us -> 72.9 us  [through(): pl.pallas_call(functools.partial(tokens_kernel, layers), grid=(tokens //...]
where the time goes in v3:
time: 308 us; the launch traced here: 307 us
  Pallas kernels  294 us (95%)
  local copies, waits for them, and re-layouts  12.8 us (4%)
    pallas_call x1, Pallas kernels, gradients(): pl.pallas_call(functools.partial(gradient_kernel, layers), out_shape=[plt...  121 us
    pallas_call x1, Pallas kernels, update(): pl.pallas_call(functools.partial(update_kernel, count, layers), out_shape...  99.6 us
    pallas_call x1, Pallas kernels, through(): pl.pallas_call(functools.partial(tokens_kernel, layers), grid=(tokens //...  72.9 us
    unnamed x19, local copies, waits for them, and re-layouts  12.8 us

profile of v3, /device:TPU:0, one launch (start us, length us, event | category | flops | bytes accessed | tf_op | source)
XLA Modules:
  0.0 307.4 jit_solution(7724686882957823424)
XLA Ops:
  0.6 72.9 %tokens.1 = (bf16[1792,2048]{1,0:T(8,128)(2,1)}, bf16[1792,2048]{1,0:T(8,128)(2,1)}, bf16[768,2048]{1,0:T(8,128)(2,1)}, bf16[768,2048]{1,0:T(8,128)(2,1)}, bf16[...) custom-call(bf16[2048,768]{1,0:T(8,128)(2,1)} %bitcast.4, ...), custom_call_target="tpu_custom_call" | custom-call | tf_op jit(solution)/shard_map/tokens/pallas_call | solution.py:561
  73.6 121.4 %gradients.1 = (bf16[2,48,1792]{2,1,0:T(8,128)(2,1)S(1)}, bf16[2,48,1792]{2,1,0:T(8,128)(2,1)S(1)}, bf16[2,112,768]{2,1,0:T(8,128)(2,1)S(1)}) custom-call(bf16[1792,2048]{1,0:T(8,128)(2,1)} %get-tuple-element.21.refs_0_, bf16[1792,2048]{1,0:T(8,128)(2,1)} %get-tuple-element.22.refs_1_, bf16[768,2048]{1,0:T(8,128)(2,1)} %get-tuple-element.23.refs_2_, ...), custom_call_target="tpu_custom_call" | custom-call | tf_op jit(solution)/shard_map/gradients/pallas_call | solution.py:445
  195.0 99.6 %update.1 = (bf16[2,768,1792]{2,1,0:T(8,128)(2,1)S(1)}, bf16[2,768,1792]{2,1,0:T(8,128)(2,1)S(1)}, bf16[2,1792,768]{2,1,0:T(8,128)(2,1)S(1)}, f32[2,48,1792]{2,1...) custom-call(bf16[2,48,1792]{2,1,0:T(8,128)(2,1)S(1)} %get-tuple-elem, ...), custom_call_target="tpu_custom_call" | custom-call | tf_op jit(solution)/shard_map/update/pallas_call | solution.py:205
  294.6 2.4 copy.29
  297.1 2.4 copy.30
  299.5 0.0 copy-start.4
  299.5 0.0 copy-start.3
  299.5 0.0 copy-start.2
  299.5 0.0 copy-start.1
  299.5 2.8 copy.31
  302.3 0.0 copy-start
  302.3 0.8 copy.32
  303.2 0.0 copy-done.4
  303.2 0.8 copy.33
  304.0 0.0 copy-done.3
  304.0 0.8 copy.34
  304.9 0.0 copy-done.2
  304.9 0.8 copy.35
  305.7 0.0 copy-done.1
  305.7 0.8 copy.36
  306.6 0.0 copy-done
  306.6 0.8 copy.37
Async XLA Ops:
  299.5 3.7 %copy-start.4 = (f32[2,48,1792]{2,1,0:T(8,128)S(1)}, f32[2,48,1792]{2,1,0:T(8,128)}, u32[]{:S(2)}) copy-start(f32[2,48,1792]{2,1,0:T(8,128)} %get-tuple-element.55) | copy-start | bytes 2064388
  299.5 4.5 %copy-start.3 = (f32[2,112,768]{2,1,0:T(8,128)S(1)}, f32[2,112,768]{2,1,0:T(8,128)}, u32[]{:S(2)}) copy-start(f32[2,112,768]{2,1,0:T(8,128)} %get-tuple-element.56) | copy-start | bytes 2064388
  299.5 5.4 %copy-start.2 = (f32[2,48,1792]{2,1,0:T(8,128)S(1)}, f32[2,48,1792]{2,1,0:T(8,128)}, u32[]{:S(2)}) copy-start(f32[2,48,1792]{2,1,0:T(8,128)} %get-tuple-element.57) | copy-start | bytes 2064388
  299.5 6.2 %copy-start.1 = (f32[2,48,1792]{2,1,0:T(8,128)S(1)}, f32[2,48,1792]{2,1,0:T(8,128)}, u32[]{:S(2)}) copy-start(f32[2,48,1792]{2,1,0:T(8,128)} %get-tuple-element.58) | copy-start | bytes 2064388
  302.3 4.3 %copy-start = (f32[2,112,768]{2,1,0:T(8,128)S(1)}, f32[2,112,768]{2,1,0:T(8,128)}, u32[]{:S(2)}) copy-start(f32[2,112,768]{2,1,0:T(8,128)} %get-tuple-element.59) | copy-start | bytes 2064388

commit v4 on v3

--- a/solution.py
+++ b/solution.py
@@ -356,16 +356,19 @@
 
             by_rows(total.shape[0], add)
 
-    def step3(k):
-        for n in range(Z - 1):
-            mine, total = gather(k, n)
-            also(k, jnp.logical_not(end), piece(n))
-
-            def store(at):
-                mine[at, :] = total[at, :].astype(BF16)
-
-            by_rows(mine.shape[0], store)
-            pass_on(k, n).start()
+    def step3(k, ends, places=(0, 1, 2)):
+        @pl.when(end if ends else jnp.logical_not(end))
+        def _():
+            for n in places:
+                mine, total = gather(k, n)
+                if not ends:
+                    also(k, z >= 0, piece(n))
+
+                def store(at):
+                    mine[at, :] = total[at, :].astype(BF16)
+
+                by_rows(mine.shape[0], store)
+                pass_on(k, n).start()
 
     def step4(k):
         i, l, _ = units[k]
@@ -411,18 +414,24 @@
         else:
             unit(k, 0, 3)
             step2(k - 1)
+            if k > 3:
+                step3(k - 4, False, (0,))
             unit(k, 3, tiles[k])
             step1(k, 0)
             step1(k, 1)
-        if k in (3, 4):
-            step3(k - 3)
+            if k > 3:
+                step3(k - 4, False, (1, 2))
+            if k > 2:
+                step3(k - 3, True)
     last = len(units) - 1
     step2(last)
-    for k in range(2, len(units)):
-        step3(k)
-        step4(k - 2)
-    step4(last - 1)
-    step4(last)
+    step3(last - 3, False)
+    for k in range(last - 2, len(units)):
+        step3(k, True)
+        step3(k, False)
+        step4(k - 3)
+    for k in range(last - 2, len(units)):
+        step4(k)
     for k in range(len(units)):
         for n in range(Z):
             swap(k, 0, n).wait_send()

time: 308 us -> 303 us (0.984)
  Pallas kernels: 294 us -> 289 us
    pallas_call x1, Pallas kernels: 121 us -> 116 us  [gradients(): pl.pallas_call(functools.partial(gradient_kernel, layers), out_shape=[plt...]
where the time goes in v4:
time: 303 us; the launch traced here: 302 us
  Pallas kernels  289 us (95%)
  local copies, waits for them, and re-layouts  12.8 us (4%)
    pallas_call x1, Pallas kernels, gradients(): pl.pallas_call(functools.partial(gradient_kernel, layers), out_shape=[plt...  116 us
    pallas_call x1, Pallas kernels, update(): pl.pallas_call(functools.partial(update_kernel, count, layers), out_shape...  99.6 us
    pallas_call x1, Pallas kernels, through(): pl.pallas_call(functools.partial(tokens_kernel, layers), grid=(tokens //...  72.9 us
    unnamed x19, local copies, waits for them, and re-layouts  12.8 us

profile of v4, /device:TPU:0, one launch (start us, length us, event | category | flops | bytes accessed | tf_op | source)
XLA Modules:
  0.0 302.1 jit_solution(3534588541584529749)
XLA Ops:
  0.6 72.9 %tokens.1 = (bf16[1792,2048]{1,0:T(8,128)(2,1)}, bf16[1792,2048]{1,0:T(8,128)(2,1)}, bf16[768,2048]{1,0:T(8,128)(2,1)}, bf16[768,2048]{1,0:T(8,128)(2,1)}, bf16[...) custom-call(bf16[2048,768]{1,0:T(8,128)(2,1)} %bitcast.4, ...), custom_call_target="tpu_custom_call" | custom-call | tf_op jit(solution)/shard_map/tokens/pallas_call | solution.py:570
  73.6 116.1 %gradients.1 = (bf16[2,48,1792]{2,1,0:T(8,128)(2,1)S(1)}, bf16[2,48,1792]{2,1,0:T(8,128)(2,1)S(1)}, bf16[2,112,768]{2,1,0:T(8,128)(2,1)S(1)}) custom-call(bf16[1792,2048]{1,0:T(8,128)(2,1)} %get-tuple-element.21.refs_0_, bf16[1792,2048]{1,0:T(8,128)(2,1)} %get-tuple-element.22.refs_1_, bf16[768,2048]{1,0:T(8,128)(2,1)} %get-tuple-element.23.refs_2_, ...), custom_call_target="tpu_custom_call" | custom-call | tf_op jit(solution)/shard_map/gradients/pallas_call | solution.py:454
  189.7 99.6 %update.1 = (bf16[2,768,1792]{2,1,0:T(8,128)(2,1)S(1)}, bf16[2,768,1792]{2,1,0:T(8,128)(2,1)S(1)}, bf16[2,1792,768]{2,1,0:T(8,128)(2,1)S(1)}, f32[2,48,1792]{2,1...) custom-call(bf16[2,48,1792]{2,1,0:T(8,128)(2,1)S(1)} %get-tuple-elem, ...), custom_call_target="tpu_custom_call" | custom-call | tf_op jit(solution)/shard_map/update/pallas_call | solution.py:205
  289.3 2.4 copy.29
  291.8 2.4 copy.30
  294.2 0.0 copy-start.4
  294.2 0.0 copy-start.3
  294.2 0.0 copy-start.2
  294.2 0.0 copy-start.1
  294.2 2.8 copy.31
  297.0 0.0 copy-start
  297.0 0.8 copy.32
  297.9 0.0 copy-done.4
  297.9 0.8 copy.33
  298.7 0.0 copy-done.3
  298.7 0.8 copy.34
  299.6 0.0 copy-done.2
  299.6 0.8 copy.35
  300.4 0.0 copy-done.1
  300.4 0.8 copy.36
  301.3 0.0 copy-done
  301.3 0.8 copy.37
Async XLA Ops:
  294.2 3.7 %copy-start.4 = (f32[2,48,1792]{2,1,0:T(8,128)S(1)}, f32[2,48,1792]{2,1,0:T(8,128)}, u32[]{:S(2)}) copy-start(f32[2,48,1792]{2,1,0:T(8,128)} %get-tuple-element.55) | copy-start | bytes 2064388
  294.2 4.5 %copy-start.3 = (f32[2,112,768]{2,1,0:T(8,128)S(1)}, f32[2,112,768]{2,1,0:T(8,128)}, u32[]{:S(2)}) copy-start(f32[2,112,768]{2,1,0:T(8,128)} %get-tuple-element.56) | copy-start | bytes 2064388
  294.2 5.4 %copy-start.2 = (f32[2,48,1792]{2,1,0:T(8,128)S(1)}, f32[2,48,1792]{2,1,0:T(8,128)}, u32[]{:S(2)}) copy-start(f32[2,48,1792]{2,1,0:T(8,128)} %get-tuple-element.57) | copy-start | bytes 2064388
  294.2 6.2 %copy-start.1 = (f32[2,48,1792]{2,1,0:T(8,128)S(1)}, f32[2,48,1792]{2,1,0:T(8,128)}, u32[]{:S(2)}) copy-start(f32[2,48,1792]{2,1,0:T(8,128)} %get-tuple-element.58) | copy-start | bytes 2064388
  297.0 4.3 %copy-start = (f32[2,112,768]{2,1,0:T(8,128)S(1)}, f32[2,112,768]{2,1,0:T(8,128)}, u32[]{:S(2)}) copy-start(f32[2,112,768]{2,1,0:T(8,128)} %get-tuple-element.59) | copy-start | bytes 2064388
